TPU v7x, 128 devices: a whole 4x4x4 slice. The times are simulated.
128 devices in a mesh: band: 32 (over z, y, x_hi), grid: 4 (over x_lo, core).
Axes of the slice: x: 4 (x_hi: 2, x_lo: 2; x = x_hi * 2 + x_lo), y: 4, z: 4, core: 2. Of those that a mesh axis runs over, the one named last changes fastest.
Arguments:
- orbitals: float32 [128, 110592], P('band', 'grid'), may hold values from -6 to 6
Outputs:
- exchange_vectors: float32 [128, 110592], P('band', 'grid')
- margin: float32 [128, 128], P('grid', 'band')
All inputs are finite; a program needn't handle non-finite values.
Results may differ from a plain program's by a relative error of at most 0.00012.
Values sent between devices are 32-bit elements; how exact they have to be, the bound alone decides.
A program may use at most 128 MiB of HBM per device.

v0:
```python
import functools
import numpy as np
import jax
import jax.numpy as jnp
from jax import lax
from jax.experimental import pallas as pl
from jax.experimental.pallas import tpu as pltpu
from jax.sharding import PartitionSpec as P

NG = 48
NCELL = 110592
BF = jnp.bfloat16
F32 = jnp.float32


def split_np(a):
    hi = a.astype(BF)
    lo = (a - hi.astype(np.float64)).astype(BF)
    return hi, lo


def tables():
    n = np.arange(NG)
    ang = 2.0 * np.pi * ((n[:, None] * n[None, :]) % NG) / NG
    h = np.cos(ang) + np.sin(ang)
    w = np.zeros((8, NG, 6, 8, 8))
    for y in range(8):
        w[y, :, :, y, :] = h.reshape(NG, 6, 8)
    w = w.reshape(384, 384)
    v = np.kron(h, np.eye(8))
    f = ((n + 24) % 48 - 24).astype(np.float64)
    q = f[:, None, None] ** 2 + f[None, :, None] ** 2 + f[None, None, :] ** 2
    k = np.where(q > 0, 40.0 * (1.0 - np.exp(-q / 16.0)) / np.where(q > 0, q, 1.0), 0.0) / NCELL
    k = k.reshape(NG, NG, 6, 8).transpose(2, 0, 1, 3).reshape(288, 384)

    def pack(m):
        hi, lo = split_np(m)
        return np.concatenate([hi, hi, lo], axis=0)

    hh, hl = split_np(h)
    hx = np.concatenate([hh, hh, hl], axis=1)
    return pack(w), pack(v), pack(w.T.copy()), hx, k.astype(np.float32)


def hilo(x):
    hi = x.astype(BF)
    lo = (x - hi.astype(F32)).astype(BF)
    return hi, lo


def put(s_ref, row, rows, lane, x):
    hi, lo = hilo(x)
    n = x.shape[1]
    s_ref[row : row + rows, lane : lane + n] = hi
    s_ref[row : row + rows, 384 + lane : 384 + lane + n] = lo


def mm3(s_ref, w_ref):
    return jnp.dot(s_ref[...], w_ref[0:768, :], preferred_element_type=F32) + jnp.dot(
        s_ref[:, 0:384], w_ref[768:1152, :], preferred_element_type=F32
    )


def swap(t_ref, s_ref, pb, left):
    for p in range(pb):
        for j in range(3):
            for m in range(3):
                r0 = p * 288 + 2 * j * 48
                e = t_ref[r0 : r0 + 48, 128 * m : 128 * m + 128]
                o = t_ref[r0 + 48 : r0 + 96, 128 * m : 128 * m + 128]
                d0 = p * 288 + 2 * m * 48
                put(s_ref, d0, 48, 128 * j, jnp.where(left, e, pltpu.roll(o, 64, 1)))
                put(s_ref, d0 + 48, 48, 128 * j, jnp.where(left, pltpu.roll(e, 64, 1), o))


def potential(pb, s_ref, t_ref, r_ref, w_ref, v_ref, wt_ref, hx_ref, k_ref):
    left = lax.broadcasted_iota(jnp.int32, (48, 128), 1) < 64
    t_ref[...] = mm3(s_ref, w_ref)
    swap(t_ref, s_ref, pb, left)
    t_ref[...] = mm3(s_ref, v_ref)
    h2 = hx_ref[:, 0:96]
    h1 = hx_ref[:, 96:144]

    def xdot(row):
        return jnp.dot(h2, r_ref[row : row + 96, :], preferred_element_type=F32) + jnp.dot(
            h1, r_ref[row : row + 48, :], preferred_element_type=F32
        )

    for i in range(pb * 6):
        hi, lo = hilo(t_ref[i * 48 : i * 48 + 48, :])
        r_ref[i * 192 : i * 192 + 48, :] = hi
        r_ref[i * 192 + 48 : i * 192 + 96, :] = lo
        z = i % 6
        d = xdot(i * 192) * k_ref[z * 48 : z * 48 + 48, :]
        hi, lo = hilo(d)
        r_ref[i * 192 + 96 : i * 192 + 144, :] = hi
        r_ref[i * 192 + 144 : i * 192 + 192, :] = lo
        put(s_ref, i * 48, 48, 0, xdot(i * 192 + 96))
    t_ref[...] = mm3(s_ref, v_ref)
    swap(t_ref, s_ref, pb, left)
    t_ref[...] = mm3(s_ref, wt_ref)


def solve_kernel(pb, idx_ref, own_ref, low_ref, w_ref, v_ref, wt_ref, hx_ref, k_ref, u_out, o_out, a_ref, u_ref, s_ref, t_ref, r_ref):
    for r in range(18):
        for xg in range(6):
            row, lane = (r // 3) * 48 + xg * 8, (r % 3) * 128
            for b in range(4):
                a_ref[b, row : row + 8, lane : lane + 128] = own_ref[pl.ds((xg * 144 + r) * 4 + b, 8, stride=72), :]
            a_ref[4, row : row + 8, lane : lane + 128] = low_ref[pl.ds(xg * 144 + r, 8, stride=18), :]
    u_ref[...] = jnp.zeros_like(u_ref)

    def step(n, carry):
        for p in range(pb):
            i, j = idx_ref[n * pb + p, 0], idx_ref[n * pb + p, 1]
            put(s_ref, p * 288, 288, 0, a_ref[i] * a_ref[j])
        potential(pb, s_ref, t_ref, r_ref, w_ref, v_ref, wt_ref, hx_ref, k_ref)
        for p in range(pb):
            i, j = idx_ref[n * pb + p, 0], idx_ref[n * pb + p, 1]
            use = idx_ref[n * pb + p, 2].astype(F32)
            other = idx_ref[n * pb + p, 3].astype(F32)
            t = t_ref[p * 288 : p * 288 + 288, :]
            u_ref[i] = u_ref[i] - use * a_ref[j] * t
            u_ref[j] = u_ref[j] - other * a_ref[i] * t
        return carry

    lax.fori_loop(0, 8 // pb, step, 0)
    for r in range(18):
        for xg in range(6):
            row, lane = (r // 3) * 48 + xg * 8, (r % 3) * 128
            for b in range(4):
                u_out[pl.ds((xg * 144 + r) * 4 + b, 8, stride=72), :] = u_ref[b, row : row + 8, lane : lane + 128]
            o_out[pl.ds(xg * 144 + r, 8, stride=18), :] = u_ref[4, row : row + 8, lane : lane + 128]


def solve(idx, own, low, pb=2):
    w, v, wt, hx, k = tables()
    vm = pl.BlockSpec(memory_space=pltpu.VMEM)
    return pl.pallas_call(
        functools.partial(solve_kernel, pb),
        out_shape=(jax.ShapeDtypeStruct((3456, 128), F32), jax.ShapeDtypeStruct((864, 128), F32)),
        in_specs=[pl.BlockSpec(memory_space=pltpu.SMEM)] + [vm] * 7,
        out_specs=(vm, vm),
        scratch_shapes=[
            pltpu.VMEM((5, 288, 384), F32),
            pltpu.VMEM((5, 288, 384), F32),
            pltpu.VMEM((pb * 288, 768), BF),
            pltpu.VMEM((pb * 288, 384), F32),
            pltpu.VMEM((pb * 6 * 192, 384), BF),
        ],
        compiler_params=pltpu.CompilerParams(vmem_limit_bytes=60 * 1024 * 1024),
    )(idx, own, low, w, v, wt, hx, k)


N_GRID = 4


def own_pairs(g):
    table = np.array(
        [
            [(0, 0, 1, 0), (1, 1, 1, 0), (0, 1, 1, 1), (0, 0, 0, 0)],
            [(2, 2, 1, 0), (0, 2, 1, 1), (0, 0, 0, 0), (0, 0, 0, 0)],
            [(3, 3, 1, 0), (2, 3, 1, 1), (1, 3, 1, 1), (0, 0, 0, 0)],
            [(0, 3, 1, 1), (1, 2, 1, 1), (0, 0, 0, 0), (0, 0, 0, 0)],
        ],
        np.int32,
    )
    cross = np.array([(i, 4, 1, 1) for i in range(4)], np.int32)
    return jnp.concatenate([cross, lax.dynamic_index_in_dim(jnp.asarray(table), g, 0, False)], axis=0)


def cut_along(shard, dim, length):
    lengths = shard.shape
    pieces = shard.reshape(*lengths[:dim], length, lengths[dim] // length, *lengths[dim + 1 :])
    return jnp.moveaxis(pieces, dim, 0)


def sent_and_summed(shard, axis, dim):
    length = lax.axis_size(axis)
    pieces = lax.all_to_all(cut_along(shard, dim, length), axis, 0, 0, tiled=True)
    return jnp.sum(pieces, axis=0)


def on_device(orbitals):
    g = lax.axis_index("grid")
    nb = lax.axis_size("band")
    mine = orbitals.reshape(4, 216, 128).transpose(1, 0, 2).reshape(864, 128)
    own = lax.all_gather(mine, "grid", axis=0, tiled=True)
    send = lax.dynamic_index_in_dim(own.reshape(864, 4, 128), g, 1, False)
    up = [(b * 4 + k, (b + 1) % nb * 4 + (k + 2) % 4) for b in range(nb) for k in range(4)]
    down = [(t, s) for s, t in up]
    low = lax.ppermute(send, ("band", "grid"), up)
    u, o = solve(own_pairs(g), own, low)
    owed = lax.ppermute(o, ("band", "grid"), down)
    mark = (jnp.arange(4) == g).astype(F32)
    total = u.reshape(864, 4, 128) + owed[:, None, :] * mark[None, :, None]
    parts = lax.all_to_all(total.reshape(4, 864, 128), "grid", 0, 0, tiled=True)
    vec = jnp.sum(parts, axis=0)
    vectors = vec.reshape(216, 4, 128).transpose(1, 0, 2).reshape(4, 27648)
    every = lax.all_gather(orbitals, "band", axis=0, tiled=True)
    margin = sent_and_summed(
        lax.dot_general(
            every, vectors, (((1,), (1,)), ((), ())), precision=lax.Precision.HIGHEST, preferred_element_type=F32
        )
        / NCELL,
        "grid",
        0,
    )
    return vectors, margin


def solution(mesh):
    return jax.shard_map(
        on_device,
        mesh=mesh,
        in_specs=(P("band", "grid"),),
        out_specs=(P("band", "grid"), P("grid", "band")),
        check_vma=False,
    )
```

profile of v0, /device:TPU:1, one launch (start us, length us, event | category | flops | bytes accessed | tf_op | source)
XLA Modules:
  0.0 241.3 jit_solution(2187201304525498338)
XLA Ops:
  7.2 0.0 copy-start.3
  7.2 0.0 all-gather.4.cloned.1.call-start
  7.2 0.7 all-gather.4.cloned.1.call-update
  7.9 0.0 all-gather.6.cloned.1.call-start
  8.0 0.7 all-gather.6.cloned.1.call-update
  8.7 31.0 %all-gather.4.cloned.1.call-done.own_ref = f32[3456,128]{1,0:T(8,128)} async-done(((f32[864,128]{1,0:T(8,128)}), f32[3456,128]{1,0:T(8,128)}) %all-gather.4.cloned.1.call-update) | async-done | bytes 1769488 | tf_op jit(solution)/shard_map/all_gather | solution.py:188
  39.7 1.9 constant_dynamic-slice_fusion
  41.5 1.9 collective-permute-start
  43.4 0.7 dynamic-slice_bitcast_fusion
  44.1 0.0 copy-done.3
  44.1 0.6 pad_add_fusion.idx_ref
  44.7 14.1 %collective-permute-done.low_ref = f32[864,128]{1,0:T(8,128)S(1)} collective-permute-done((f32[864,128]{1,0:T(8,128)S(1)}, f32[864,128]{1,0:T(8,128)S(1)}, u32[]{:S(2)}, u32[]{:S(2)}) %collective-permute-start) | collective-permute-done | bytes 442400 | tf_op jit(solution)/shard_map/ppermute | solution.py:192
  58.7 0.0 copy-start.2
  58.8 0.8 copy-done.2
  59.5 28.0 %shard_map.95 = (f32[3456,128]{1,0:T(8,128)}, f32[864,128]{1,0:T(8,128)}) custom-call(s32[8,4]{1,0:T(8,128)} %pad_add_fusion.idx_ref, f32[3456,128]{1,0:T(8,128)} %all-gather.4.cloned.1.call-done.own_ref, f32[864,128]{1,0:T(8,128)} %copy-done.2, bf16[1152,384]{1,0:T(8,128)(2,1)} %constant.35.clone.w_ref, bf16[1152,384]{1,0:T(8,128)(2,1)} %constant.36.clone.v_ref, ...), custom_call_target="tpu_custom_call" | custom-call | tf_op jit(solution)/shard_map/pallas_call | solution.py:139
  87.5 0.0 copy-start.1
  87.5 2.2 collective-permute-start.1
  89.7 0.1 mul.23
  89.9 12.0 %collective-permute-done.1 = f32[864,128]{1,0:T(8,128)S(1)} collective-permute-done((f32[864,128]{1,0:T(8,128)}, f32[864,128]{1,0:T(8,128)S(1)}, u32[]{:S(2)}, u32[]{:S(2)}) %collective-permute-start.1) | collective-permute-done | bytes 442400 | tf_op jit(solution)/shard_map/ppermute | solution.py:194
  101.9 0.3 mul.20
  102.2 0.0 copy-done.1
  102.2 0.3 fusion
  102.6 33.2 %all_to_all.10 = f32[4,864,128]{2,1,0:T(8,128)S(1)} all-to-all(f32[4,864,128]{2,1,0:T(8,128)S(1)} %fusion), channel_id=1, replica_groups=mesh['band'=32,'grid'=4] {'grid'}, dimensions={0} | all-to-all | bytes 3538944 | tf_op jit(solution)/shard_map/all_to_all | solution.py:197
  135.8 0.1 reduce_sum.18
  135.9 0.0 copy-start
  135.9 62.4 %all-gather.6.cloned.1.call-done = f32[32,4,27648]{2,1,0:T(4,128)} async-done(((f32[1,4,27648]{2,1,0:T(4,128)}), f32[32,4,27648]{2,1,0:T(4,128)}) %all-gather.6.cloned.1.call-update) | async-done | bytes 14155792 | tf_op jit(solution)/shard_map/all_gather | solution.py:200
  198.3 14.1 %reshape.44 = f32[128,27648]{1,0:T(8,128)} reshape(f32[32,4,27648]{2,1,0:T(4,128)} %all-gather.6.cloned.1.call-done) | data formatting | bytes 28311552
  212.3 0.0 copy-done
  212.4 13.6 %fusion.1 = f32[128,4]{0,1:T(4,128)S(1)} fusion(f32[4,27648]{1,0:T(4,128)S(1)} %bitcast.36, f32[128,27648]{1,0:T(8,128)} %reshape.44), kind=kOutput, calls=%fused_computation.3 | convolution fusion | flops 169869824 | bytes 14600192 | tf_op jit(solution)/shard_map/dot_general | solution.py:202
  226.0 0.1 reshape.42
  226.0 0.1 reshape.45
  226.1 6.5 %all_to_all.11 = f32[4,1,128]{2,1,0:T(1,128)S(1)} all-to-all(f32[4,1,128]{2,1,0:T(1,128)S(1)} %reshape.45), channel_id=1, replica_groups=mesh['band'=32,'grid'=4] {'grid'}, dimensions={0} | all-to-all | bytes 4096 | tf_op jit(solution)/shard_map/all_to_all | solution.py:180
  232.6 0.5 broadcast.14
  233.2 0.7 reduce
  233.8 0.1 reshape.46
  233.9 0.6 bitcast_reduce_fusion
  (3 shorter events, 0.0 us)
Async XLA Ops:
  7.2 36.9 %copy-start.3 = (s32[4,4]{1,0:T(4,128)S(1)}, s32[4,4]{1,0:T(4,128)}, u32[]{:S(2)}) copy-start(s32[4,4]{1,0:T(4,128)} %constant.34.clone) | copy-start | bytes 196
  7.2 32.5 %all-gather.4.cloned.1.call-start = ((), (), s32[]{:S(2)}) async-start(), calls=%async_computation.2 | async-start | bytes 2211840 | tf_op jit(solution)/shard_map/all_gather | solution.py:188
  7.9 190.4 %all-gather.6.cloned.1.call-start = ((), (), s32[]{:S(2)}) async-start(), calls=%async_computation.3 | async-start | bytes 14598144 | tf_op jit(solution)/shard_map/all_gather | solution.py:200
  41.5 17.2 %collective-permute-start = (f32[864,128]{1,0:T(8,128)S(1)}, f32[864,128]{1,0:T(8,128)S(1)}, u32[]{:S(2)}, u32[]{:S(2)}) collective-permute-start(f32[864,128]{1,0:T(8,128)S(1)} %bitcast.41), channel_id=1, source_target_pairs={{0,6},{1,7},{2,4},{3,5},{4,10},{5,11},{6,8},{7,9},{8,14},{9,15},{1... | collective-permute-start | bytes 1327112 | tf_op jit(solution)/shard_map/ppermute | solution.py:192
  58.7 0.8 copy-start.2
  87.5 14.7 %copy-start.1 = (f32[3456,128]{1,0:T(8,128)S(1)}, f32[3456,128]{1,0:T(8,128)}, u32[]{:S(2)}) copy-start(f32[3456,128]{1,0:T(8,128)} %get-tuple-element.4) | copy-start | bytes 5308420
  87.5 14.4 %collective-permute-start.1 = (f32[864,128]{1,0:T(8,128)}, f32[864,128]{1,0:T(8,128)S(1)}, u32[]{:S(2)}, u32[]{:S(2)}) collective-permute-start(f32[864,128]{1,0:T(8,128)} %get-tuple-element.5), channel_id=1, source_target_pairs={{6,0},{7,1},{4,2},{5,3},{10,4},{11,5},{8,6},{9,7},{14,8},{15,9},{1... | collective-permute-start | bytes 1327112 | tf_op jit(solution)/shard_map/ppermute | solution.py:194
  135.9 76.5 %copy-start = (f32[864,128]{1,0:T(8,128)}, f32[864,128]{1,0:T(8,128)S(1)}, u32[]{:S(2)}) copy-start(f32[864,128]{1,0:T(8,128)S(1)} %reduce_sum.18) | copy-start | bytes 1327108
Sparse Core Ops, SparseCore 0:
  9.6 29.9 all-gather.3
  42.7 155.5 all-gather.5
where the time goes:
time: 242 us; the launch traced here: 241 us
  waiting for transfers between devices  121 us (50%)
  blocking collectives  39.7 us (16%)
  Pallas kernels  28 us (12%)
  local copies, waits for them, and re-layouts  18.6 us (8%)
  between operations  14.1 us (6%)
  matrix products  13.6 us (6%)
  starting transfers between devices  4.13 us (2%)
    all_gather x1, waiting for transfers between devices, on_device(): every = lax.all_gather(orbitals, 'band', axis=0, tiled=True)  62.4 us
    all_to_all x1, blocking collectives, on_device(): parts = lax.all_to_all(total.reshape(4, 864, 128), 'grid', 0, 0, tiled=True)  33.2 us
    all_gather x1, waiting for transfers between devices, on_device(): own = lax.all_gather(mine, 'grid', axis=0, tiled=True)  31 us
    pallas_call x1, Pallas kernels, solve(): pl.pallas_call(functools.partial(solve_kernel, pb), out_shape=(jax.ShapeD...  28 us
    unnamed x11, local copies, waits for them, and re-layouts  15 us
    ppermute x1, waiting for transfers between devices, on_device(): low = lax.ppermute(send, ('band', 'grid'), up)  14.1 us
    dot_general x1, matrix products, on_device(): lax.dot_general(every, vectors, (((1,), (1,)), ((), ())), precision=lax.P...  13.6 us
    ppermute x1, waiting for transfers between devices, on_device(): owed = lax.ppermute(o, ('band', 'grid'), down)  12 us
  transfers between devices with their start and end apart: 4, of which 4 were waited for; matrix products, arithmetic and copies ran while one was open for 2% of the time, Pallas kernels for 12%

commit v1 on v0

--- a/solution.py
+++ b/solution.py
@@ -152,6 +152,156 @@
     )(idx, own, low, w, v, wt, hx, k)
 
 
+MESH = pl.DeviceIdType.MESH
+GROUPS = 27
+HIGHEST = lax.Precision.HIGHEST
+
+
+def rcopy(src, dst, send, recv, band, grid):
+    return pltpu.make_async_remote_copy(
+        src_ref=src, dst_ref=dst, send_sem=send, recv_sem=recv, device_id={"band": band, "grid": grid}, device_id_type=MESH
+    )
+
+
+def landed(ref, sem):
+    pltpu.make_async_copy(ref, ref, sem).wait()
+
+
+def greet(nb, me, g):
+    barrier = pltpu.get_barrier_semaphore()
+
+    def one(o, c):
+        pl.semaphore_signal(barrier, inc=1, device_id={"band": (me + o) % nb, "grid": g}, device_id_type=MESH)
+        return c
+
+    lax.fori_loop(1, nb, one, 0)
+    for o in range(1, 4):
+        pl.semaphore_signal(barrier, inc=1, device_id={"band": me, "grid": (g + o) % 4}, device_id_type=MESH)
+    pl.semaphore_wait(barrier, nb + 2)
+
+
+def scatter_groups(src, buf, send, recv, nb, me, g):
+    def one(o, c):
+        dst = (me + o) % nb
+
+        @pl.when(dst < GROUPS)
+        def _():
+            rcopy(
+                src.at[pl.ds(pl.multiple_of(dst * 32, 32), 32)], buf.at[pl.ds(pl.multiple_of(me * 32, 32), 32)], send, recv, dst, g
+            ).start()
+
+        return c
+
+    lax.fori_loop(1, nb, one, 0)
+
+    @pl.when(me < GROUPS)
+    def _():
+        rows = pl.ds(pl.multiple_of(me * 32, 32), 32)
+        buf[rows, :] = src[rows, :]
+
+
+def sent_all(ref, send, me, unit):
+    @pl.when(me < GROUPS)
+    def _():
+        landed(ref.at[0 : (GROUPS - 1) * unit], send)
+
+    @pl.when(me >= GROUPS)
+    def _():
+        landed(ref.at[0 : GROUPS * unit], send)
+
+
+def margin_tail(nb, me, g, out_ref, obuf, vbuf, amat, bmat, mt8, red, gsum, rs, rr, gs, gr):
+    @pl.when(me < GROUPS)
+    def _():
+        for c in range(8):
+            for b in range(4):
+                rows = pl.ds(c * 4 + b, 32, stride=32)
+                amat[c * 128 + b * 32 : c * 128 + b * 32 + 32, :] = vbuf[rows, :]
+                bmat[pl.ds(c * 128 + b, 32, stride=4), :] = obuf[rows, :]
+        m = jnp.zeros((128, 128), F32)
+        for c in range(8):
+            part = slice(c * 128, c * 128 + 128)
+            m = m + lax.dot_general(
+                amat[part, :], bmat[part, :], (((1,), (1,)), ((), ())), precision=HIGHEST, preferred_element_type=F32
+            )
+        m = m * (1.0 / NCELL)
+        mt8[...] = jnp.zeros_like(mt8)
+        for b in range(4):
+            mt8[pl.ds(b, 32, stride=8), :] = m[b * 32 : b * 32 + 32, :]
+
+        def one(o, c):
+            dst = (me + o) % nb
+            rcopy(
+                mt8.at[pl.ds(pl.multiple_of(dst * 8, 8), 8)], red.at[pl.ds(pl.multiple_of(me * 8, 8), 8)], rs, rr, dst, g
+            ).start()
+            return c
+
+        lax.fori_loop(1, nb, one, 0)
+        rows = pl.ds(pl.multiple_of(me * 8, 8), 8)
+        red[rows, :] = mt8[rows, :]
+
+    sent_all(red, rr, me, 8)
+    total = red[0:8, :]
+    for s in range(1, GROUPS):
+        total = total + red[s * 8 : s * 8 + 8, :]
+    mine = pl.ds(pl.multiple_of(g * 8, 8), 8)
+    gsum[mine, :] = total
+    sends = [rcopy(gsum.at[mine], gsum.at[mine], gs.at[o - 1], gr.at[o - 1], me, (g + o) % 4) for o in range(1, 4)]
+    for s in sends:
+        s.start()
+    for s in sends:
+        s.wait()
+    full = gsum[0:8, :] + gsum[8:16, :] + gsum[16:24, :] + gsum[24:32, :]
+    picked = jnp.zeros((4, 32), F32)
+    for t in range(4):
+        picked = picked + jnp.where(g == t, 1.0, 0.0) * full[0:4, t * 32 : t * 32 + 32]
+    out_ref[...] = picked
+
+    @pl.when(me < GROUPS)
+    def _():
+        landed(mt8.at[0 : 31 * 8], rs)
+
+
+def margin_kernel(nb, orb_ref, vec_ref, out_ref, obuf, vbuf, amat, bmat, mt8, red, gsum, os, orr, vs, vr, rs, rr, gs, gr):
+    me, g = lax.axis_index("band"), lax.axis_index("grid")
+    greet(nb, me, g)
+    scatter_groups(orb_ref, obuf, os, orr, nb, me, g)
+    scatter_groups(vec_ref, vbuf, vs, vr, nb, me, g)
+
+    @pl.when(me < GROUPS)
+    def _():
+        landed(obuf.at[0 : 31 * 32], orr)
+        landed(vbuf.at[0 : 31 * 32], vr)
+
+    margin_tail(nb, me, g, out_ref, obuf, vbuf, amat, bmat, mt8, red, gsum, rs, rr, gs, gr)
+    sent_all(obuf, os, me, 32)
+    sent_all(vbuf, vs, me, 32)
+
+
+MARGIN_SCRATCH = [
+    pltpu.VMEM((1024, 128), F32),
+    pltpu.VMEM((1024, 128), F32),
+    pltpu.VMEM((1024, 128), F32),
+    pltpu.VMEM((1024, 128), F32),
+    pltpu.VMEM((256, 128), F32),
+    pltpu.VMEM((256, 128), F32),
+    pltpu.VMEM((32, 128), F32),
+]
+
+
+def margin_of(mine, vec, nb):
+    vm = pl.BlockSpec(memory_space=pltpu.VMEM)
+    dma = pltpu.SemaphoreType.DMA
+    return pl.pallas_call(
+        functools.partial(margin_kernel, nb),
+        out_shape=jax.ShapeDtypeStruct((4, 32), F32),
+        in_specs=[vm, vm],
+        out_specs=vm,
+        scratch_shapes=MARGIN_SCRATCH + [dma] * 6 + [dma((3,)), dma((3,))],
+        compiler_params=pltpu.CompilerParams(collective_id=3, has_side_effects=True),
+    )(mine, vec)
+
+
 N_GRID = 4
 
 
@@ -167,18 +317,6 @@
     )
     cross = np.array([(i, 4, 1, 1) for i in range(4)], np.int32)
     return jnp.concatenate([cross, lax.dynamic_index_in_dim(jnp.asarray(table), g, 0, False)], axis=0)
-
-
-def cut_along(shard, dim, length):
-    lengths = shard.shape
-    pieces = shard.reshape(*lengths[:dim], length, lengths[dim] // length, *lengths[dim + 1 :])
-    return jnp.moveaxis(pieces, dim, 0)
-
-
-def sent_and_summed(shard, axis, dim):
-    length = lax.axis_size(axis)
-    pieces = lax.all_to_all(cut_along(shard, dim, length), axis, 0, 0, tiled=True)
-    return jnp.sum(pieces, axis=0)
 
 
 def on_device(orbitals):
@@ -197,15 +335,7 @@
     parts = lax.all_to_all(total.reshape(4, 864, 128), "grid", 0, 0, tiled=True)
     vec = jnp.sum(parts, axis=0)
     vectors = vec.reshape(216, 4, 128).transpose(1, 0, 2).reshape(4, 27648)
-    every = lax.all_gather(orbitals, "band", axis=0, tiled=True)
-    margin = sent_and_summed(
-        lax.dot_general(
-            every, vectors, (((1,), (1,)), ((), ())), precision=lax.Precision.HIGHEST, preferred_element_type=F32
-        )
-        / NCELL,
-        "grid",
-        0,
-    )
+    margin = margin_of(mine, vec, nb).T
     return vectors, margin
 
 

time: 242 us -> 166 us (0.69)
  waiting for transfers between devices: 121 us -> 55.9 us
  Pallas kernels: 28 us -> 58.9 us
  blocking collectives: 39.7 us -> 25.6 us
  local copies, waits for them, and re-layouts: 18.6 us -> 4.99 us
  matrix products: 13.6 us -> 0 us
    all_gather x1 -> x0, waiting for transfers between devices: 62.4 us -> none  [on_device(): every = lax.all_gather(orbitals, 'band', axis=0, tiled=True)]
    pallas_call x0 -> x1, Pallas kernels: none -> 31 us  [margin_of(): pl.pallas_call(functools.partial(margin_kernel, nb), out_shape=jax.ShapeD...]
    dot_general x1 -> x0, matrix products: 13.6 us -> none  [on_device(): lax.dot_general(every, vectors, (((1,), (1,)), ((), ())), precision=lax.P...]
    unnamed x11 -> x5, local copies, waits for them, and re-layouts: 15 us -> 2.03 us
    all_to_all x1, blocking collectives: 33.2 us -> 25.6 us  [on_device(): parts = lax.all_to_all(total.reshape(4, 864, 128), 'grid', 0, 0, tiled=True)]
    all_to_all x1 -> x0, blocking collectives: 6.5 us -> none  [sent_and_summed(): lax.all_to_all(cut_along(shard, dim, length), axis, 0, 0, tiled=True)]
  transfers between devices with their start and end apart: 4 -> 3, of which waited for: 4 -> 3; matrix products, arithmetic and copies ran while one was open for 2% -> 1% of each run, Pallas kernels for 12% -> 0%
where the time goes in v1:
time: 166 us
  Pallas kernels  58.9 us (35%)
  waiting for transfers between devices  55.9 us (34%)
  blocking collectives  25.6 us (15%)
  between operations  14.1 us (8%)
  local copies, waits for them, and re-layouts  4.99 us (3%)
  starting transfers between devices  4.04 us (2%)
  other arithmetic  2.5 us (2%)
    all_gather x1, waiting for transfers between devices, on_device(): own = lax.all_gather(mine, 'grid', axis=0, tiled=True)  31.7 us
    pallas_call x1, Pallas kernels, margin_of(): pl.pallas_call(functools.partial(margin_kernel, nb), out_shape=jax.ShapeD...  31 us
    pallas_call x1, Pallas kernels, solve(): pl.pallas_call(functools.partial(solve_kernel, pb), out_shape=(jax.ShapeD...  27.9 us
    all_to_all x1, blocking collectives, on_device(): parts = lax.all_to_all(total.reshape(4, 864, 128), 'grid', 0, 0, tiled=True)  25.6 us
    ppermute x1, waiting for transfers between devices, on_device(): low = lax.ppermute(send, ('band', 'grid'), up)  13.4 us
    ppermute x1, waiting for transfers between devices, on_device(): owed = lax.ppermute(o, ('band', 'grid'), down)  10 us
  transfers between devices with their start and end apart: 3, of which 3 were waited for; matrix products, arithmetic and copies ran while one was open for 1% of the time, Pallas kernels for 0%

profile of v1, /device:TPU:1, one launch (start us, length us, event | category | flops | bytes accessed | tf_op | source)
XLA Modules:
  0.0 166.0 jit_solution(8498667611393237184)
XLA Ops:
  7.2 0.0 all-gather.2.cloned.1.call-start
  7.2 0.7 all-gather.2.cloned.1.call-update
  7.9 31.7 %all-gather.2.cloned.1.call-done.own_ref = f32[3456,128]{1,0:T(8,128)} async-done(((f32[864,128]{1,0:T(8,128)}), f32[3456,128]{1,0:T(8,128)}) %all-gather.2.cloned.1.call-update) | async-done | bytes 1769488 | tf_op jit(solution)/shard_map/all_gather | solution.py:326
  39.7 1.9 %constant_dynamic-slice_fusion = f32[864,1,128]{2,1,0:T(1,128)S(1)} fusion(f32[864,4,128]{2,1,0:T(4,128)} %bitcast.22, s32[]{:T(128)S(6)} %select_n.6), kind=kLoop, calls=%fused_computation.5 | loop fusion | bytes 884740 | tf_op jit(solution)/shard_map/jit(dynamic_index_in_dim)/dynamic_slice | solution.py:327
  41.5 1.9 %collective-permute-start = (f32[864,128]{1,0:T(8,128)S(1)}, f32[864,128]{1,0:T(8,128)S(1)}, u32[]{:S(2)}, u32[]{:S(2)}) collective-permute-start(f32[864,128]{1,0:T(8,128)S(1)} %bitcast.27), channel_id=1, source_target_pairs={{0,6},{1,7},{2,4},{3,5},{4,10},{5,11},{6,8},{7,9},{8,14},{9,15},{1... | collective-permute-start | bytes 1327112 | tf_op jit(solution)/shard_map/ppermute | solution.py:330
  43.4 0.7 dynamic-slice_bitcast_fusion
  44.1 1.3 pad_add_fusion.idx_ref
  45.3 13.4 %collective-permute-done.low_ref = f32[864,128]{1,0:T(8,128)S(1)} collective-permute-done((f32[864,128]{1,0:T(8,128)S(1)}, f32[864,128]{1,0:T(8,128)S(1)}, u32[]{:S(2)}, u32[]{:S(2)}) %collective-permute-start) | collective-permute-done | bytes 442400 | tf_op jit(solution)/shard_map/ppermute | solution.py:330
  58.7 0.0 copy-start.1
  58.7 0.8 copy-done.1
  59.5 27.9 %shard_map.95 = (f32[3456,128]{1,0:T(8,128)}, f32[864,128]{1,0:T(8,128)}) custom-call(s32[8,4]{1,0:T(8,128)} %pad_add_fusion.idx_ref, f32[3456,128]{1,0:T(8,128)} %all-gather.2.cloned.1.call-done.own_ref, f32[864,128]{1,0:T(8,128)} %copy-done.1, bf16[1152,384]{1,0:T(8,128)(2,1)} %constant.32.clone.w_ref, bf16[1152,384]{1,0:T(8,128)(2,1)} %constant.33.clone.v_ref, ...), custom_call_target="tpu_custom_call" | custom-call | tf_op jit(solution)/shard_map/pallas_call | solution.py:139
  87.4 0.0 copy-start
  87.4 2.1 %collective-permute-start.1 = (f32[864,128]{1,0:T(8,128)}, f32[864,128]{1,0:T(8,128)S(1)}, u32[]{:S(2)}, u32[]{:S(2)}) collective-permute-start(f32[864,128]{1,0:T(8,128)} %get-tuple-element.5), channel_id=1, source_target_pairs={{6,0},{7,1},{4,2},{5,3},{10,4},{11,5},{8,6},{9,7},{14,8},{15,9},{1... | collective-permute-start | bytes 1327112 | tf_op jit(solution)/shard_map/ppermute | solution.py:332
  89.6 0.1 mul.23
  89.7 10.0 %collective-permute-done.1 = f32[864,128]{1,0:T(8,128)S(1)} collective-permute-done((f32[864,128]{1,0:T(8,128)}, f32[864,128]{1,0:T(8,128)S(1)}, u32[]{:S(2)}, u32[]{:S(2)}) %collective-permute-start.1) | collective-permute-done | bytes 442400 | tf_op jit(solution)/shard_map/ppermute | solution.py:332
  99.7 0.3 mul.20
  100.0 0.0 copy-done
  100.1 0.3 fusion
  100.4 25.6 %all_to_all.5 = f32[4,864,128]{2,1,0:T(8,128)S(1)} all-to-all(f32[4,864,128]{2,1,0:T(8,128)S(1)} %fusion), channel_id=1, replica_groups=mesh['band'=32,'grid'=4] {'grid'}, dimensions={0} | all-to-all | bytes 3538944 | tf_op jit(solution)/shard_map/all_to_all | solution.py:335
  126.0 0.9 reduce_sum.9.vec_ref
  126.8 31.0 %shard_map.96 = f32[4,32]{1,0:T(4,128)} custom-call(f32[864,128]{1,0:T(8,128)} %bitcast.25, f32[864,128]{1,0:T(8,128)} %reduce_sum.9.vec_ref), custom_call_target="tpu_custom_call" | custom-call | tf_op jit(solution)/shard_map/pallas_call | solution.py:295
  157.9 1.3 copy.15
  (2 shorter events, 0.0 us)
Async XLA Ops:
  7.2 32.5 %all-gather.2.cloned.1.call-start = ((), (), s32[]{:S(2)}) async-start(), calls=%async_computation.1 | async-start | bytes 2211840 | tf_op jit(solution)/shard_map/all_gather | solution.py:326
  41.5 17.2 %collective-permute-start = (f32[864,128]{1,0:T(8,128)S(1)}, f32[864,128]{1,0:T(8,128)S(1)}, u32[]{:S(2)}, u32[]{:S(2)}) collective-permute-start(f32[864,128]{1,0:T(8,128)S(1)} %bitcast.27), channel_id=1, source_target_pairs={{0,6},{1,7},{2,4},{3,5},{4,10},{5,11},{6,8},{7,9},{8,14},{9,15},{1... | collective-permute-start | bytes 1327112 | tf_op jit(solution)/shard_map/ppermute | solution.py:330
  58.7 0.8 copy-start.1
  87.4 12.6 %copy-start = (f32[3456,128]{1,0:T(8,128)S(1)}, f32[3456,128]{1,0:T(8,128)}, u32[]{:S(2)}) copy-start(f32[3456,128]{1,0:T(8,128)} %get-tuple-element.4) | copy-start | bytes 5308420
  87.4 12.3 %collective-permute-start.1 = (f32[864,128]{1,0:T(8,128)}, f32[864,128]{1,0:T(8,128)S(1)}, u32[]{:S(2)}, u32[]{:S(2)}) collective-permute-start(f32[864,128]{1,0:T(8,128)} %get-tuple-element.5), channel_id=1, source_target_pairs={{6,0},{7,1},{4,2},{5,3},{10,4},{11,5},{8,6},{9,7},{14,8},{15,9},{1... | collective-permute-start | bytes 1327112 | tf_op jit(solution)/shard_map/ppermute | solution.py:332
Sparse Core Ops, SparseCore 0:
  9.6 29.9 all-gather.1

commit v2 on v1

v2 whole, which is shorter than its diff:
```python
import functools
import numpy as np
import jax
import jax.numpy as jnp
from jax import lax
from jax.experimental import pallas as pl
from jax.experimental.pallas import tpu as pltpu
from jax.sharding import PartitionSpec as P

NG = 48
NCELL = 110592
BF = jnp.bfloat16
F32 = jnp.float32


def split_np(a):
    hi = a.astype(BF)
    lo = (a - hi.astype(np.float64)).astype(BF)
    return hi, lo


def tables():
    n = np.arange(NG)
    ang = 2.0 * np.pi * ((n[:, None] * n[None, :]) % NG) / NG
    h = np.cos(ang) + np.sin(ang)
    w = np.zeros((8, NG, 6, 8, 8))
    for y in range(8):
        w[y, :, :, y, :] = h.reshape(NG, 6, 8)
    w = w.reshape(384, 384)
    v = np.kron(h, np.eye(8))
    f = ((n + 24) % 48 - 24).astype(np.float64)
    q = f[:, None, None] ** 2 + f[None, :, None] ** 2 + f[None, None, :] ** 2
    k = np.where(q > 0, 40.0 * (1.0 - np.exp(-q / 16.0)) / np.where(q > 0, q, 1.0), 0.0) / NCELL
    k = k.reshape(NG, NG, 6, 8).transpose(2, 0, 1, 3).reshape(288, 384)

    def pack(m):
        hi, lo = split_np(m)
        return np.concatenate([hi, hi, lo], axis=0)

    hh, hl = split_np(h)
    hx = np.concatenate([hh, hh, hl], axis=1)
    return pack(w), pack(v), pack(w.T.copy()), hx, k.astype(np.float32)


def hilo(x):
    hi = x.astype(BF)
    lo = (x - hi.astype(F32)).astype(BF)
    return hi, lo


def put(s_ref, row, rows, lane, x):
    hi, lo = hilo(x)
    n = x.shape[1]
    s_ref[row : row + rows, lane : lane + n] = hi
    s_ref[row : row + rows, 384 + lane : 384 + lane + n] = lo


def mm3(s_ref, w_ref):
    return jnp.dot(s_ref[...], w_ref[0:768, :], preferred_element_type=F32) + jnp.dot(
        s_ref[:, 0:384], w_ref[768:1152, :], preferred_element_type=F32
    )


def swap(t_ref, s_ref, pb, left):
    for p in range(pb):
        for j in range(3):
            for m in range(3):
                r0 = p * 288 + 2 * j * 48
                e = t_ref[r0 : r0 + 48, 128 * m : 128 * m + 128]
                o = t_ref[r0 + 48 : r0 + 96, 128 * m : 128 * m + 128]
                d0 = p * 288 + 2 * m * 48
                put(s_ref, d0, 48, 128 * j, jnp.where(left, e, pltpu.roll(o, 64, 1)))
                put(s_ref, d0 + 48, 48, 128 * j, jnp.where(left, pltpu.roll(e, 64, 1), o))


def potential(pb, s_ref, t_ref, r_ref, w_ref, v_ref, wt_ref, hx_ref, k_ref):
    left = lax.broadcasted_iota(jnp.int32, (48, 128), 1) < 64
    t_ref[...] = mm3(s_ref, w_ref)
    swap(t_ref, s_ref, pb, left)
    t_ref[...] = mm3(s_ref, v_ref)
    h2 = hx_ref[:, 0:96]
    h1 = hx_ref[:, 96:144]

    def xdot(row):
        return jnp.dot(h2, r_ref[row : row + 96, :], preferred_element_type=F32) + jnp.dot(
            h1, r_ref[row : row + 48, :], preferred_element_type=F32
        )

    for i in range(pb * 6):
        hi, lo = hilo(t_ref[i * 48 : i * 48 + 48, :])
        r_ref[i * 192 : i * 192 + 48, :] = hi
        r_ref[i * 192 + 48 : i * 192 + 96, :] = lo
        z = i % 6
        d = xdot(i * 192) * k_ref[z * 48 : z * 48 + 48, :]
        hi, lo = hilo(d)
        r_ref[i * 192 + 96 : i * 192 + 144, :] = hi
        r_ref[i * 192 + 144 : i * 192 + 192, :] = lo
        put(s_ref, i * 48, 48, 0, xdot(i * 192 + 96))
    t_ref[...] = mm3(s_ref, v_ref)
    swap(t_ref, s_ref, pb, left)
    t_ref[...] = mm3(s_ref, wt_ref)


MESH = pl.DeviceIdType.MESH
GROUPS = 27
HIGHEST = lax.Precision.HIGHEST
QR = 864
PARTS = 3
PR = QR // PARTS


def rcopy(src, dst, send, recv, band, grid):
    return pltpu.make_async_remote_copy(
        src_ref=src, dst_ref=dst, send_sem=send, recv_sem=recv, device_id={"band": band, "grid": grid}, device_id_type=MESH
    )


def landed(ref, sem):
    pltpu.make_async_copy(ref, ref, sem).wait()


def greet(nb, me, g):
    barrier = pltpu.get_barrier_semaphore()

    def signal(band, grid):
        pl.semaphore_signal(barrier, inc=1, device_id={"band": band, "grid": grid}, device_id_type=MESH)

    def one(o, c):
        signal((me + o) % nb, g)
        return c

    signal((me + 1) % nb, (g + 2) % 4)
    signal((me + nb - 1) % nb, (g + 2) % 4)
    for o in range(1, 4):
        signal(me, (g + o) % 4)
    lax.fori_loop(1, nb, one, 0)
    pl.semaphore_wait(barrier, nb + 4)


def span(start, size):
    return pl.ds(pl.multiple_of(start, 8), size)


def scatter_groups(src, buf, send, recv, nb, me, g):
    def one(o, c):
        dst = (me + o) % nb

        @pl.when(dst < GROUPS)
        def _():
            rcopy(src.at[span(dst * 32, 32)], buf.at[span(me * 32, 32)], send, recv, dst, g).start()

        return c

    lax.fori_loop(1, nb, one, 0)

    @pl.when(me < GROUPS)
    def _():
        buf[span(me * 32, 32), :] = src[span(me * 32, 32), :]


def sent_all(ref, sem, me, unit):
    @pl.when(me < GROUPS)
    def _():
        landed(ref.at[0 : (GROUPS - 1) * unit], sem)

    @pl.when(me >= GROUPS)
    def _():
        landed(ref.at[0 : GROUPS * unit], sem)


def margin_tail(nb, me, g, out_ref, obuf, vbuf, amat, bmat, mt8, red, gsum, rs, rr, gs, gr):
    @pl.when(me < GROUPS)
    def _():
        for c in range(8):
            for b in range(4):
                rows = pl.ds(c * 4 + b, 32, stride=32)
                amat[c * 128 + b * 32 : c * 128 + b * 32 + 32, :] = vbuf[rows, :]
                bmat[pl.ds(c * 128 + b, 32, stride=4), :] = obuf[rows, :]
        m = jnp.zeros((128, 128), F32)
        for c in range(8):
            part = slice(c * 128, c * 128 + 128)
            m = m + lax.dot_general(
                amat[part, :], bmat[part, :], (((1,), (1,)), ((), ())), precision=HIGHEST, preferred_element_type=F32
            )
        m = m * (1.0 / NCELL)
        mt8[...] = jnp.zeros_like(mt8)
        for b in range(4):
            mt8[pl.ds(b, 32, stride=8), :] = m[b * 32 : b * 32 + 32, :]

        def one(o, c):
            dst = (me + o) % nb
            rcopy(mt8.at[span(dst * 8, 8)], red.at[span(me * 8, 8)], rs, rr, dst, g).start()
            return c

        lax.fori_loop(1, nb, one, 0)
        red[span(me * 8, 8), :] = mt8[span(me * 8, 8), :]

    sent_all(red, rr, me, 8)
    total = red[0:8, :]
    for s in range(1, GROUPS):
        total = total + red[s * 8 : s * 8 + 8, :]
    mine = span(g * 8, 8)
    gsum[mine, :] = total
    sends = [rcopy(gsum.at[mine], gsum.at[mine], gs.at[o - 1], gr.at[o - 1], me, (g + o) % 4) for o in range(1, 4)]
    for s in sends:
        s.start()
    for s in sends:
        s.wait()
    full = gsum[0:8, :] + gsum[8:16, :] + gsum[16:24, :] + gsum[24:32, :]
    picked = jnp.zeros((4, 32), F32)
    for t in range(4):
        picked = picked + jnp.where(g == t, 1.0, 0.0) * full[0:4, t * 32 : t * 32 + 32]
    out_ref[...] = picked

    @pl.when(me < GROUPS)
    def _():
        landed(mt8.at[0 : 31 * 8], rs)


OWN_I = ((0, 1, 0), (2, 0, 0), (3, 2, 1), (0, 1, 0))
OWN_J = ((0, 1, 1), (2, 2, 0), (3, 3, 3), (3, 2, 0))
OWN_N = (3, 2, 3, 2)


def chosen(g, values):
    total = 0
    for t, value in enumerate(values):
        total = total + jnp.where(g == t, value, 0)
    return total


def whole_kernel(
    nb,
    mine,
    w_hbm,
    v_hbm,
    wt_hbm,
    hx_hbm,
    k_hbm,
    vec_out,
    m_out,
    w_ref,
    v_ref,
    wt_ref,
    hx_ref,
    k_ref,
    own,
    low,
    a_ref,
    u_ref,
    s_ref,
    t_ref,
    r_ref,
    un,
    on,
    ow,
    sb,
    xr,
    obuf,
    vbuf,
    amat,
    bmat,
    mt8,
    red,
    gsum,
    tab,
    sib_s,
    sib_r,
    cross_s,
    cross_r,
    fwd_s,
    fwd_r,
    low_s,
    low_r,
    ow_s,
    ow_r,
    sb_s,
    sb_r,
    xr_s,
    xr_r,
    os,
    orr,
    vs,
    vr,
    rs,
    rr,
    gs,
    gr,
):
    me, g = lax.axis_index("band"), lax.axis_index("grid")
    c, s = (g + 2) % 4, g + 1 - 2 * (g % 2)
    cs = (s + 2) % 4
    up, down = (me + 1) % nb, (me + nb - 1) % nb
    loads = [
        pltpu.make_async_copy(a, b, tab.at[n])
        for n, (a, b) in enumerate(
            ((w_hbm, w_ref), (v_hbm, v_ref), (wt_hbm, wt_ref), (hx_hbm, hx_ref), (k_hbm, k_ref))
        )
    ]
    for copy in loads:
        copy.start()
    greet(nb, me, g)

    own3, mine3 = own.reshape(864, 4, 128), mine.reshape(216, 4, 128)

    cross = [
        rcopy(mine.at[span(n * PR, PR)], own.at[span(g * QR + n * PR, PR)], cross_s.at[n], cross_r.at[n], me, c)
        for n in range(PARTS)
    ]
    for copy in cross:
        copy.start()
    sib = rcopy(mine, own.at[span(g * QR, QR)], sib_s, sib_r, me, s)
    sib.start()
    rcopy(mine3.at[:, g, :], low.at[span(g * 216, 216)], low_s, low_r, up, c).start()
    own[span(g * QR, QR), :] = mine[...]

    def low_part(start, size):
        rcopy(own3.at[pl.ds(start, size), g, :], low.at[span(start, size)], low_s, low_r, up, c).start()

    landed(own.at[span(s * QR, QR)], sib_r)
    low_part(s * 216, 216)
    scatter_groups(mine, obuf, os, orr, nb, me, g)
    fwd = []
    for n in range(PARTS):
        part = own.at[span(c * QR + n * PR, PR)]
        landed(part, cross_r.at[n])
        copy = rcopy(part, part, fwd_s.at[n], fwd_r.at[n], me, s)
        copy.start()
        fwd.append(copy)
        low_part(c * 216 + n * 72, 72)
    for n in range(PARTS):
        landed(own.at[span(cs * QR + n * PR, PR)], fwd_r.at[n])
        low_part(cs * 216 + n * 72, 72)

    for r in range(18):
        for xg in range(6):
            row, lane = (r // 3) * 48 + xg * 8, (r % 3) * 128
            for b in range(4):
                a_ref[b, row : row + 8, lane : lane + 128] = own[pl.ds((xg * 144 + r) * 4 + b, 8, stride=72), :]
    u_ref[...] = jnp.zeros_like(u_ref)
    for copy in loads:
        copy.wait()

    def pair(i, j, other):
        put(s_ref, 0, 288, 0, a_ref[i] * a_ref[j])
        potential(1, s_ref, t_ref, r_ref, w_ref, v_ref, wt_ref, hx_ref, k_ref)
        t = t_ref[...]
        u_ref[i] = u_ref[i] - a_ref[j] * t
        u_ref[j] = u_ref[j] - other * a_ref[i] * t

    def own_pair(n, carry):
        i = chosen(g, [row[0] for row in OWN_I])
        j = chosen(g, [row[0] for row in OWN_J])
        for slot in (1, 2):
            i = jnp.where(n == slot, chosen(g, [row[slot] for row in OWN_I]), i)
            j = jnp.where(n == slot, chosen(g, [row[slot] for row in OWN_J]), j)
        pair(i, j, jnp.where(i == j, 0.0, 1.0))
        return carry

    def cross_pair(n, carry):
        pair(n, 4, 1.0)
        return carry

    lax.fori_loop(0, 1, own_pair, 0)
    landed(low, low_r)
    for r in range(18):
        for xg in range(6):
            row, lane = (r // 3) * 48 + xg * 8, (r % 3) * 128
            a_ref[4, row : row + 8, lane : lane + 128] = low[pl.ds(xg * 144 + r, 8, stride=18), :]
    lax.fori_loop(0, 4, cross_pair, 0)

    for r in range(18):
        for xg in range(6):
            row, lane = (r // 3) * 48 + xg * 8, (r % 3) * 128
            on[pl.ds(xg * 144 + r, 8, stride=18), :] = u_ref[4, row : row + 8, lane : lane + 128]
    back = []
    for n, q in enumerate((s, g, cs, c)):
        part = span(q * 216, 216)
        copy = rcopy(on.at[part], ow.at[part], ow_s.at[n], ow_r.at[n], down, c)
        copy.start()
        back.append(copy)
    lax.fori_loop(1, chosen(g, OWN_N), own_pair, 0)

    for r in range(18):
        for xg in range(6):
            row, lane = (r // 3) * 48 + xg * 8, (r % 3) * 128
            for b in range(4):
                un[pl.ds((xg * 144 + r) * 4 + b, 8, stride=72), :] = u_ref[b, row : row + 8, lane : lane + 128]

    def add_owed(n, q):
        landed(ow.at[span(q * 216, 216)], ow_r.at[n])

        def rows(t, carry):
            to = pl.ds(q * QR + t * 32 + g, 8, stride=4)
            un[to, :] = un[to, :] + ow[span(q * 216 + t * 8, 8), :]
            return carry

        lax.fori_loop(0, 27, rows, 0)

    add_owed(0, cs)
    pass_on = [rcopy(un.at[span(q * QR, QR)], sb.at[n], sb_s.at[n], sb_r.at[n], me, s) for n, q in enumerate((cs, s))]
    pass_on[0].start()
    add_owed(1, c)
    landed(sb.at[0], sb_r.at[0])
    away = []
    for n in range(PARTS):
        part = span(c * QR + n * PR, PR)
        un[part, :] = un[part, :] + sb[0, n * PR : n * PR + PR, :]
        copy = rcopy(un.at[part], xr.at[span(n * PR, PR)], xr_s.at[n], xr_r.at[n], me, c)
        copy.start()
        away.append(copy)
    add_owed(2, s)
    pass_on[1].start()
    add_owed(3, g)
    landed(sb.at[1], sb_r.at[1])
    for n in range(PARTS):
        part = slice(n * PR, n * PR + PR)
        landed(xr.at[part], xr_r.at[n])
        vec_out[part, :] = un[span(g * QR + n * PR, PR), :] + sb[1, part, :] + xr[part, :]

    scatter_groups(vec_out, vbuf, vs, vr, nb, me, g)

    @pl.when(me < GROUPS)
    def _():
        landed(obuf.at[0 : 31 * 32], orr)
        landed(vbuf.at[0 : 31 * 32], vr)

    margin_tail(nb, me, g, m_out, obuf, vbuf, amat, bmat, mt8, red, gsum, rs, rr, gs, gr)
    sent_all(obuf, os, me, 32)
    sent_all(vbuf, vs, me, 32)
    for copy in cross + fwd + [sib] + back + pass_on + away:
        copy.wait_send()
    landed(on, low_s)


def on_device(orbitals):
    nb = lax.axis_size("band")
    mine = orbitals.reshape(4, 216, 128).transpose(1, 0, 2).reshape(864, 128)
    vm = pl.BlockSpec(memory_space=pltpu.VMEM)
    hbm = pl.BlockSpec(memory_space=pl.ANY)
    dma = pltpu.SemaphoreType.DMA
    w, v, wt, hx, k = tables()

    def f32(*shape):
        return pltpu.VMEM(shape, F32)

    def b16(*shape):
        return pltpu.VMEM(shape, BF)

    vec, margin = pl.pallas_call(
        functools.partial(whole_kernel, nb),
        out_shape=(jax.ShapeDtypeStruct((864, 128), F32), jax.ShapeDtypeStruct((4, 32), F32)),
        in_specs=[vm] + [hbm] * 5,
        out_specs=(vm, vm),
        scratch_shapes=[b16(1152, 384), b16(1152, 384), b16(1152, 384), b16(48, 144), f32(288, 384)]
        + [f32(3456, 128), f32(864, 128), f32(5, 288, 384), f32(5, 288, 384)]
        + [b16(288, 768), f32(288, 384), b16(1152, 384)]
        + [f32(3456, 128), f32(864, 128), f32(864, 128), f32(2, 864, 128), f32(864, 128)]
        + [f32(1024, 128), f32(1024, 128), f32(1024, 128), f32(1024, 128), f32(256, 128), f32(256, 128), f32(32, 128)]
        + [dma((5,)), dma, dma, dma((3,)), dma((3,)), dma((3,)), dma((3,)), dma, dma]
        + [dma((4,)), dma((4,)), dma((2,)), dma((2,)), dma((3,)), dma((3,))]
        + [dma] * 6
        + [dma((3,)), dma((3,))],
        compiler_params=pltpu.CompilerParams(
            collective_id=3, has_side_effects=True, vmem_limit_bytes=60 * 1024 * 1024
        ),
    )(mine, w, v, wt, hx, k)
    return vec.reshape(216, 4, 128).transpose(1, 0, 2).reshape(4, 27648), margin.T


def solution(mesh):
    return jax.shard_map(
        on_device,
        mesh=mesh,
        in_specs=(P("band", "grid"),),
        out_specs=(P("band", "grid"), P("grid", "band")),
        check_vma=False,
    )
```

time: 166 us -> 87.6 us (0.53)
  waiting for transfers between devices: 55.9 us -> 0 us
  blocking collectives: 25.6 us -> 0 us
  Pallas kernels: 58.9 us -> 84.4 us
  between operations: 14.1 us -> 0.65 us
  starting transfers between devices: 4.04 us -> 0 us
  local copies, waits for them, and re-layouts: 4.99 us -> 2.39 us
  other arithmetic: 2.5 us -> 0 us
    all_gather x1 -> x0, waiting for transfers between devices: 31.7 us -> none  [on_device(): own = lax.all_gather(mine, 'grid', axis=0, tiled=True)]
    all_to_all x1 -> x0, blocking collectives: 25.6 us -> none  [on_device(): parts = lax.all_to_all(total.reshape(4, 864, 128), 'grid', 0, 0, tiled=True)]
    pallas_call x2 -> x1, Pallas kernels: 58.9 us -> 84.4 us  [on_device(): pl.pallas_call(functools.partial(whole_kernel, nb), out_shape=(jax.ShapeD...]
    ppermute x2 -> x0, waiting for transfers between devices: 23.4 us -> none  [the longest x1 13.4 us: on_device(): low = lax.ppermute(send, ('band', 'grid'), up)]
    ppermute x2 -> x0, starting transfers between devices: 4 us -> none  [the longest x1 2.14 us: on_device(): owed = lax.ppermute(o, ('band', 'grid'), down)]
    dynamic_slice x1 -> x0, local copies, waits for them, and re-layouts: 1.86 us -> none  [on_device(): send = lax.dynamic_index_in_dim(own.reshape(864, 4, 128), g, 1, False)]
  transfers between devices with their start and end apart: 3 -> 0, of which waited for: 3 -> 0; matrix products, arithmetic and copies ran while one was open for 1% -> 0% of each run, Pallas kernels for 0% -> 0%
where the time goes in v2:
time: 87.6 us; the launch traced here: 87.5 us
  Pallas kernels  84.4 us (96%)
  local copies, waits for them, and re-layouts  2.39 us (3%)
    pallas_call x1, Pallas kernels, on_device(): pl.pallas_call(functools.partial(whole_kernel, nb), out_shape=(jax.ShapeD...  84.4 us
    unnamed x4, local copies, waits for them, and re-layouts  2.39 us

profile of v2, /device:TPU:1, one launch (start us, length us, event | category | flops | bytes accessed | tf_op | source)
XLA Modules:
  0.0 87.5 jit_solution(13740573315878032366)
XLA Ops:
  0.6 84.4 %shard_map.77 = (f32[864,128]{1,0:T(8,128)}, f32[4,32]{1,0:T(4,128)}) custom-call(f32[864,128]{1,0:T(8,128)} %bitcast.11, bf16[1152,384]{1,0:T(8,128)(2,1)} %constant.10.clone.w_hbm, bf16[1152,384]{1,0:T(8,128)(2,1)} %constant.11.clone.v_hbm, bf16[1152,384]{1,0:T(8,128)(2,1)} %constant.12.clone.wt_hbm, bf16[48,144]{1,0:T(8,128)(2,1)} %constant.13.clone.hx_hbm, ...), custom_call_target="tpu_custom_call" | custom-call | tf_op jit(solution)/shard_map/pallas_call | solution.py:450
  85.1 0.0 copy-start
  85.1 1.8 %copy.12 = f32[4,27648]{1,0:T(4,128)} copy(f32[4,27648]{1,0:T(4,128)} %bitcast.12) | data formatting | bytes 884736
  86.9 0.0 copy-done
  86.9 0.6 copy.13
Async XLA Ops:
  85.1 1.8 %copy-start = (f32[4,32]{1,0:T(4,128)S(1)}, f32[4,32]{1,0:T(4,128)}, u32[]{:S(2)}) copy-start(f32[4,32]{1,0:T(4,128)} %get-tuple-element.5) | copy-start | bytes 1540

commit v3 on v2

v3 whole, which is shorter than its diff:
```python
import functools
import numpy as np
import jax
import jax.numpy as jnp
from jax import lax
from jax.experimental import pallas as pl
from jax.experimental.pallas import tpu as pltpu
from jax.sharding import PartitionSpec as P

NG = 48
NCELL = 110592
BF = jnp.bfloat16
F32 = jnp.float32


def split_np(a):
    hi = a.astype(BF)
    lo = (a - hi.astype(np.float64)).astype(BF)
    return hi, lo


def tables():
    n = np.arange(NG)
    ang = 2.0 * np.pi * ((n[:, None] * n[None, :]) % NG) / NG
    h = np.cos(ang) + np.sin(ang)
    w = np.zeros((8, NG, 6, 8, 8))
    for y in range(8):
        w[y, :, :, y, :] = h.reshape(NG, 6, 8)
    w = w.reshape(384, 384)
    v = np.kron(h, np.eye(8))
    f = ((n + 24) % 48 - 24).astype(np.float64)
    q = f[:, None, None] ** 2 + f[None, :, None] ** 2 + f[None, None, :] ** 2
    k = np.where(q > 0, 40.0 * (1.0 - np.exp(-q / 16.0)) / np.where(q > 0, q, 1.0), 0.0) / NCELL
    k = k.reshape(NG, NG, 6, 8).transpose(2, 0, 1, 3).reshape(288, 384)

    def pack(m):
        hi, lo = split_np(m)
        return np.concatenate([hi, lo], axis=0)

    hh, hl = split_np(h)
    hx = np.concatenate([hh, hh, hl], axis=1)
    return pack(w), pack(v), pack(w.T.copy()), hx, k.astype(np.float32)


def hilo(x):
    hi = x.astype(BF)
    lo = (x - hi.astype(F32)).astype(BF)
    return hi, lo


def put(s_ref, row, rows, lane, x):
    hi, lo = hilo(x)
    n = x.shape[1]
    s_ref[row : row + rows, lane : lane + n] = hi
    s_ref[row : row + rows, 384 + lane : 384 + lane + n] = lo


def mm3(s_ref, w_ref):
    return jnp.dot(s_ref[...], w_ref[0:768, :], preferred_element_type=F32) + jnp.dot(
        s_ref[:, 0:384], w_ref[768:1152, :], preferred_element_type=F32
    )


def swap(t_ref, s_ref, pb, left):
    for p in range(pb):
        for j in range(3):
            for m in range(3):
                r0 = p * 288 + 2 * j * 48
                e = t_ref[r0 : r0 + 48, 128 * m : 128 * m + 128]
                o = t_ref[r0 + 48 : r0 + 96, 128 * m : 128 * m + 128]
                d0 = p * 288 + 2 * m * 48
                put(s_ref, d0, 48, 128 * j, jnp.where(left, e, pltpu.roll(o, 64, 1)))
                put(s_ref, d0 + 48, 48, 128 * j, jnp.where(left, pltpu.roll(e, 64, 1), o))


def potential(pb, s_ref, t_ref, r_ref, w_ref, v_ref, wt_ref, hx_ref, k_ref):
    left = lax.broadcasted_iota(jnp.int32, (48, 128), 1) < 64
    t_ref[...] = mm3(s_ref, w_ref)
    swap(t_ref, s_ref, pb, left)
    t_ref[...] = mm3(s_ref, v_ref)
    h2 = hx_ref[:, 0:96]
    h1 = hx_ref[:, 96:144]

    def xdot(row):
        return jnp.dot(h2, r_ref[row : row + 96, :], preferred_element_type=F32) + jnp.dot(
            h1, r_ref[row : row + 48, :], preferred_element_type=F32
        )

    for i in range(pb * 6):
        hi, lo = hilo(t_ref[i * 48 : i * 48 + 48, :])
        r_ref[i * 192 : i * 192 + 48, :] = hi
        r_ref[i * 192 + 48 : i * 192 + 96, :] = lo
        z = i % 6
        d = xdot(i * 192) * k_ref[z * 48 : z * 48 + 48, :]
        hi, lo = hilo(d)
        r_ref[i * 192 + 96 : i * 192 + 144, :] = hi
        r_ref[i * 192 + 144 : i * 192 + 192, :] = lo
        put(s_ref, i * 48, 48, 0, xdot(i * 192 + 96))
    t_ref[...] = mm3(s_ref, v_ref)
    swap(t_ref, s_ref, pb, left)
    t_ref[...] = mm3(s_ref, wt_ref)


MESH = pl.DeviceIdType.MESH
GROUPS = 27
HIGHEST = lax.Precision.HIGHEST


def rcopy(src, dst, send, recv, band, grid):
    return pltpu.make_async_remote_copy(
        src_ref=src, dst_ref=dst, send_sem=send, recv_sem=recv, device_id={"band": band, "grid": grid}, device_id_type=MESH
    )


def landed(ref, sem):
    pltpu.make_async_copy(ref, ref, sem).wait()


def greet(nb, me, g):
    barrier = pltpu.get_barrier_semaphore()

    def signal(band, grid):
        pl.semaphore_signal(barrier, inc=1, device_id={"band": band, "grid": grid}, device_id_type=MESH)

    def one(o, c):
        signal((me + o) % nb, g)
        return c

    signal((me + 1) % nb, (g + 2) % 4)
    signal((me + nb - 1) % nb, (g + 2) % 4)
    for o in range(1, 4):
        signal(me, (g + o) % 4)
    lax.fori_loop(1, nb, one, 0)
    pl.semaphore_wait(barrier, nb + 4)


def span(start, size):
    return pl.ds(pl.multiple_of(start, 8), size)


def nth(g, n):
    return (n + 2 * (g // 2)) % 4


def scatter_groups(src, buf, send, recv, nb, me, g, rows=32, at=0):
    def one(o, c):
        dst = (me + o) % nb

        @pl.when(dst < GROUPS)
        def _():
            rcopy(src.at[span(dst * rows, rows)], buf.at[span(me * 32 + at, rows)], send, recv, dst, g).start()

        return c

    lax.fori_loop(1, nb, one, 0)

    @pl.when(me < GROUPS)
    def _():
        buf[span(me * 32 + at, rows), :] = src[span(me * rows, rows), :]


def sent_all(ref, sem, me, unit):
    @pl.when(me < GROUPS)
    def _():
        landed(ref.at[0 : (GROUPS - 1) * unit], sem)

    @pl.when(me >= GROUPS)
    def _():
        landed(ref.at[0 : GROUPS * unit], sem)


def margin_tail(nb, me, g, out_ref, obuf, vbuf, amat, bmat, mt8, red, gsum, rs, rr, gs, gr):
    @pl.when(me < GROUPS)
    def _():
        for c in range(8):
            for b in range(4):
                amat[c * 128 + b * 32 : c * 128 + b * 32 + 32, :] = vbuf[pl.ds(b * 8 + c, 32, stride=32), :]
                bmat[pl.ds(c * 128 + b, 32, stride=4), :] = obuf[pl.ds(c * 4 + b, 32, stride=32), :]
        m = jnp.zeros((128, 128), F32)
        for c in range(8):
            part = slice(c * 128, c * 128 + 128)
            m = m + lax.dot_general(
                amat[part, :], bmat[part, :], (((1,), (1,)), ((), ())), precision=HIGHEST, preferred_element_type=F32
            )
        m = m * (1.0 / NCELL)
        mt8[...] = jnp.zeros_like(mt8)
        for n in range(4):
            mt8[pl.ds(nth(g, n + 2), 32, stride=8), :] = m[n * 32 : n * 32 + 32, :]

        def one(o, c):
            dst = (me + o) % nb
            rcopy(mt8.at[span(dst * 8, 8)], red.at[span(me * 8, 8)], rs, rr, dst, g).start()
            return c

        lax.fori_loop(1, nb, one, 0)
        red[span(me * 8, 8), :] = mt8[span(me * 8, 8), :]

    sent_all(red, rr, me, 8)
    total = red[0:8, :]
    for s in range(1, GROUPS):
        total = total + red[s * 8 : s * 8 + 8, :]
    mine = span(g * 8, 8)
    gsum[mine, :] = total
    sends = [rcopy(gsum.at[mine], gsum.at[mine], gs.at[o - 1], gr.at[o - 1], me, (g + o) % 4) for o in range(1, 4)]
    for s in sends:
        s.start()
    for s in sends:
        s.wait()
    full = gsum[0:8, :] + gsum[8:16, :] + gsum[16:24, :] + gsum[24:32, :]
    picked = jnp.zeros((4, 32), F32)
    for t in range(4):
        picked = picked + jnp.where(g == t, 1.0, 0.0) * full[0:4, t * 32 : t * 32 + 32]
    out_ref[...] = picked

    @pl.when(me < GROUPS)
    def _():
        landed(mt8.at[0 : 31 * 8], rs)


OWN_I = ((0, 0, 1), (0, 1, 0), (2, 2, 3), (2, 3, 0))
OWN_J = ((0, 2, 1), (1, 3, 0), (2, 1, 3), (3, 0, 0))
STEPS = (7, 6, 7, 6)


def chosen(g, values):
    total = 0
    for t, value in enumerate(values):
        total = total + jnp.where(g == t, value, 0)
    return total


def whole_kernel(nb, mine, w_hbm, v_hbm, wt_hbm, hx_hbm, k_hbm, vec_out, m_out, *scratch):
    (w_ref, v_ref, wt_ref, hx_ref, k_ref, own, low, a_ref, u_ref, s_ref, t_ref, r_ref, un, on, ow, sb, xr, stage) = scratch[:18]
    (obuf, vbuf, amat, bmat, mt8, red, gsum, tab, sib_s, sib_r, cross_s, cross_r, fwd_s, fwd_r) = scratch[18:32]
    (low_s, low_r, ow_s, ow_r, sb_s, sb_r, xr_s, xr_r, os, orr, vs, vr, vs2, vr2, rs, rr, gs, gr) = scratch[32:]
    me, g = lax.axis_index("band"), lax.axis_index("grid")
    c, s = (g + 2) % 4, g + 1 - 2 * (g % 2)
    cs = (s + 2) % 4
    up, down = (me + 1) % nb, (me + nb - 1) % nb
    loads = []
    for n, (a, b) in enumerate(((w_hbm, w_ref), (v_hbm, v_ref), (wt_hbm, wt_ref))):
        loads.append(pltpu.make_async_copy(a.at[0:384], b.at[0:384], tab.at[2 * n]))
        loads.append(pltpu.make_async_copy(a, b.at[384:1152], tab.at[2 * n + 1]))
    loads.append(pltpu.make_async_copy(hx_hbm, hx_ref, tab.at[6]))
    loads.append(pltpu.make_async_copy(k_hbm, k_ref, tab.at[7]))
    for copy in loads:
        copy.start()
    greet(nb, me, g)

    mine3 = mine.reshape(216, 4, 128)

    def cells(ref, b, q):
        return ref.at[span(b * 864 + q * 216, 216)]

    cross = []
    for n in range(4):
        b = nth(c, n)
        cross.append(rcopy(mine3.at[:, b, :], cells(own, b, g), cross_s.at[n], cross_r.at[n], me, c))
        cross[n].start()
    sib = []
    for b in range(4):
        sib.append(rcopy(mine3.at[:, b, :], cells(own, b, g), sib_s.at[b], sib_r.at[b], me, s))
        sib[b].start()
    rcopy(mine3.at[:, g, :], low.at[span(g * 216, 216)], low_s, low_r, up, c).start()

    def spread(t, carry):
        for b in range(4):
            own[span(b * 864 + g * 216 + t * 8, 8), :] = mine[pl.ds(t * 32 + b, 8, stride=4), :]
        return carry

    lax.fori_loop(0, 27, spread, 0)

    def low_part(q):
        rcopy(cells(own, g, q), low.at[span(q * 216, 216)], low_s, low_r, up, c).start()

    for b in range(4):
        landed(cells(own, b, s), sib_r.at[b])
    low_part(s)
    fwd = [
        rcopy(cells(own, nth(g, n), c), cells(own, nth(g, n), c), fwd_s.at[n], fwd_r.at[n], me, s) for n in range(4)
    ]

    def crossed(n):
        landed(cells(own, nth(g, n), c), cross_r.at[n])
        fwd[n].start()

    def forwarded(n):
        landed(cells(own, nth(g, n), cs), fwd_r.at[n])

    def spread_low(n):
        @pl.when(g % 2 == n)
        def _():
            low_part(c)

    def spread_low2(n):
        @pl.when(g % 2 == n)
        def _():
            low_part(cs)

    for n in range(2):
        crossed(n)
        spread_low(n)
    for n in range(2):
        forwarded(n)
        spread_low2(n)
    u_ref[...] = jnp.zeros_like(u_ref)
    for copy in loads:
        copy.wait()

    def lay(slot, src, base):
        for r in range(18):
            for xg in range(6):
                row, lane = (r // 3) * 48 + xg * 8, (r % 3) * 128
                a_ref[slot, row : row + 8, lane : lane + 128] = src[pl.ds(base + xg * 144 + r, 8, stride=18), :]

    def unlay(slot, dst, base):
        for r in range(18):
            for xg in range(6):
                row, lane = (r // 3) * 48 + xg * 8, (r % 3) * 128
                dst[pl.ds(base + xg * 144 + r, 8, stride=18), :] = u_ref[slot, row : row + 8, lane : lane + 128]

    def lay_band(n):
        b = nth(g, n)
        lay(b, own, b * 864)

    def unlay_band(n):
        b = nth(g, n)
        unlay(b, un, b * 864)

    lay_band(0)
    lay_band(1)

    back = [
        rcopy(on.at[span(q * 216, 216)], ow.at[span(q * 216, 216)], ow_s.at[n], ow_r.at[n], down, c)
        for n, q in enumerate((s, g, cs, c))
    ]
    pass_on = []
    for n in range(4):
        for h, q in enumerate((cs, s)):
            at = n * 2 + h
            pass_on.append(
                rcopy(cells(un, nth(g, n), q), sb.at[at * 216 : at * 216 + 216], sb_s.at[at], sb_r.at[at], me, s)
            )
    away = [
        rcopy(cells(un, nth(g, n), c), xr.at[(n ^ 2) * 216 : (n ^ 2) * 216 + 216], xr_s.at[n], xr_r.at[n ^ 2], me, c)
        for n in range(4)
    ]

    def send_away(n):
        at = n * 2
        landed(sb.at[at * 216 : at * 216 + 216], sb_r.at[at])
        part = span(nth(g, n) * 864 + c * 216, 216)
        un[part, :] = un[part, :] + sb[at * 216 : at * 216 + 216, :]
        away[n].start()

    def step(n, carry):
        @pl.when(n == 1)
        def _():
            crossed(2)
            landed(low, low_r)
            lay(4, low, 0)
            scatter_groups(mine, obuf, os, orr, nb, me, g)

        @pl.when(n == 2)
        def _():
            crossed(3)

        @pl.when(n == 3)
        def _():
            forwarded(2)
            forwarded(3)
            lay_band(2)
            lay_band(3)

        @pl.when(n == 6)
        def _():
            early()

        i, j, other = 0, 4, 1.0
        for at, slot in ((0, 0), (3, 1), (6, 2)):
            i = jnp.where(n == at, chosen(g, [row[slot] for row in OWN_I]), i)
            j = jnp.where(n == at, chosen(g, [row[slot] for row in OWN_J]), j)
        for at, k in ((1, 0), (2, 1), (4, 2), (5, 3)):
            i = jnp.where(n == at, nth(g, k), i)
        other = jnp.where(i == j, 0.0, 1.0)
        put(s_ref, 0, 288, 0, a_ref[i] * a_ref[j])
        potential(1, s_ref, t_ref, r_ref, w_ref, v_ref, wt_ref, hx_ref, k_ref)
        t = t_ref[...]
        u_ref[i] = u_ref[i] - a_ref[j] * t
        u_ref[j] = u_ref[j] - other * a_ref[i] * t
        return carry

    def early():
        unlay(4, on, 0)
        for copy in back:
            copy.start()
        for n in (2, 3):
            unlay_band(n)
            pass_on[2 * n].start()
            pass_on[2 * n + 1].start()
        send_away(2)
        send_away(3)

    lax.fori_loop(0, 6, step, 0)

    @pl.when(g % 2 == 1)
    def _():
        early()

    lax.fori_loop(6, chosen(g, STEPS), step, 0)

    for n in (0, 1):
        unlay_band(n)

    def add_owed(n, q):
        landed(ow.at[span(q * 216, 216)], ow_r.at[n])
        part = span(g * 864 + q * 216, 216)
        un[part, :] = un[part, :] + ow[span(q * 216, 216), :]

    def finish(n, at, rows):
        b = nth(g, n)
        landed(sb.at[(n * 2 + 1) * 216 : (n * 2 + 2) * 216], sb_r.at[n * 2 + 1])
        landed(xr.at[n * 216 : n * 216 + 216], xr_r.at[n])

        def group(t, carry):
            value = (
                un[span(b * 864 + g * 216 + t * 8, 8), :]
                + sb[span((n * 2 + 1) * 216 + t * 8, 8), :]
                + xr[span(n * 216 + t * 8, 8), :]
            )
            vec_out[pl.ds(t * 32 + b, 8, stride=4), :] = value
            stage[span(rows + t * 16 + at * 8, 8), :] = value
            return carry

        lax.fori_loop(0, 27, group, 0)

    add_owed(0, cs)
    pass_on[0].start()
    pass_on[2].start()
    add_owed(1, c)
    send_away(0)
    send_away(1)
    add_owed(2, s)
    pass_on[1].start()
    pass_on[3].start()
    finish(2, 0, 0)
    finish(3, 1, 0)
    scatter_groups(stage.at[0:432], vbuf, vs, vr, nb, me, g, 16, 0)
    add_owed(3, g)
    finish(0, 0, 432)
    finish(1, 1, 432)
    scatter_groups(stage.at[432:864], vbuf, vs2, vr2, nb, me, g, 16, 16)

    @pl.when(me < GROUPS)
    def _():
        landed(obuf.at[0 : 31 * 32], orr)
        landed(vbuf.at[0 : 31 * 16], vr)
        landed(vbuf.at[0 : 31 * 16], vr2)

    margin_tail(nb, me, g, m_out, obuf, vbuf, amat, bmat, mt8, red, gsum, rs, rr, gs, gr)
    sent_all(obuf, os, me, 32)
    sent_all(obuf, vs, me, 16)
    sent_all(obuf, vs2, me, 16)
    for copy in cross + fwd + sib + back + pass_on + away:
        copy.wait_send()
    landed(on, low_s)


def on_device(orbitals):
    nb = lax.axis_size("band")
    mine = orbitals.reshape(4, 216, 128).transpose(1, 0, 2).reshape(864, 128)
    vm = pl.BlockSpec(memory_space=pltpu.VMEM)
    hbm = pl.BlockSpec(memory_space=pl.ANY)
    dma = pltpu.SemaphoreType.DMA
    w, v, wt, hx, k = tables()

    def f32(*shape):
        return pltpu.VMEM(shape, F32)

    def b16(*shape):
        return pltpu.VMEM(shape, BF)

    vec, margin = pl.pallas_call(
        functools.partial(whole_kernel, nb),
        out_shape=(jax.ShapeDtypeStruct((864, 128), F32), jax.ShapeDtypeStruct((4, 32), F32)),
        in_specs=[vm] + [hbm] * 5,
        out_specs=(vm, vm),
        scratch_shapes=[b16(1152, 384), b16(1152, 384), b16(1152, 384), b16(48, 144), f32(288, 384)]
        + [f32(3456, 128), f32(864, 128), f32(5, 288, 384), f32(5, 288, 384)]
        + [b16(288, 768), f32(288, 384), b16(1152, 384)]
        + [f32(3456, 128), f32(864, 128), f32(864, 128), f32(1728, 128), f32(864, 128), f32(864, 128)]
        + [f32(1024, 128), f32(1024, 128), f32(1024, 128), f32(1024, 128), f32(256, 128), f32(256, 128), f32(32, 128)]
        + [dma((8,)), dma((4,)), dma((4,)), dma((4,)), dma((4,)), dma((4,)), dma((4,)), dma, dma]
        + [dma((4,)), dma((4,)), dma((8,)), dma((8,)), dma((4,)), dma((4,))]
        + [dma] * 8
        + [dma((3,)), dma((3,))],
        compiler_params=pltpu.CompilerParams(
            collective_id=3, has_side_effects=True, vmem_limit_bytes=60 * 1024 * 1024
        ),
    )(mine, w, v, wt, hx, k)
    return vec.reshape(216, 4, 128).transpose(1, 0, 2).reshape(4, 27648), margin.T


def solution(mesh):
    return jax.shard_map(
        on_device,
        mesh=mesh,
        in_specs=(P("band", "grid"),),
        out_specs=(P("band", "grid"), P("grid", "band")),
        check_vma=False,
    )
```

time: 87.6 us -> 78.4 us (0.89)
  Pallas kernels: 84.4 us -> 75.1 us
    pallas_call x1, Pallas kernels: 84.4 us -> 75.1 us  [on_device(): pl.pallas_call(functools.partial(whole_kernel, nb), out_shape=(jax.ShapeD...]
where the time goes in v3:
time: 78.4 us; the launch traced here: 78.2 us
  Pallas kernels  75.1 us (96%)
  local copies, waits for them, and re-layouts  2.39 us (3%)
    pallas_call x1, Pallas kernels, on_device(): pl.pallas_call(functools.partial(whole_kernel, nb), out_shape=(jax.ShapeD...  75.1 us
    unnamed x4, local copies, waits for them, and re-layouts  2.39 us

profile of v3, /device:TPU:1, one launch (start us, length us, event | category | flops | bytes accessed | tf_op | source)
XLA Modules:
  0.0 78.2 jit_solution(605662814822623256)
XLA Ops:
  0.6 75.1 %shard_map.77 = (f32[864,128]{1,0:T(8,128)}, f32[4,32]{1,0:T(4,128)}) custom-call(f32[864,128]{1,0:T(8,128)} %bitcast.12, bf16[768,384]{1,0:T(8,128)(2,1)} %constant.10.clone.w_hbm, bf16[768,384]{1,0:T(8,128)(2,1)} %constant.11.clone.v_hbm, bf16[768,384]{1,0:T(8,128)(2,1)} %constant.12.clone.wt_hbm, bf16[48,144]{1,0:T(8,128)(2,1)} %constant.13.clone.hx_hbm, ...), custom_call_target="tpu_custom_call" | custom-call | tf_op jit(solution)/shard_map/pallas_call | solution.py:483
  75.8 0.0 copy-start
  75.8 1.8 %copy.12 = f32[4,27648]{1,0:T(4,128)} copy(f32[4,27648]{1,0:T(4,128)} %bitcast.11) | data formatting | bytes 884736
  77.6 0.0 copy-done
  77.6 0.6 copy.13
Async XLA Ops:
  75.8 1.8 %copy-start = (f32[4,32]{1,0:T(4,128)S(1)}, f32[4,32]{1,0:T(4,128)}, u32[]{:S(2)}) copy-start(f32[4,32]{1,0:T(4,128)} %get-tuple-element.5) | copy-start | bytes 1540

commit v4 on v3

--- a/solution.py
+++ b/solution.py
@@ -102,8 +102,6 @@
 
 
 MESH = pl.DeviceIdType.MESH
-GROUPS = 27
-HIGHEST = lax.Precision.HIGHEST
 
 
 def rcopy(src, dst, send, recv, band, grid):
@@ -118,20 +116,22 @@
 
 def greet(nb, me, g):
     barrier = pltpu.get_barrier_semaphore()
+    plane, w = me // 8, me % 8
 
     def signal(band, grid):
         pl.semaphore_signal(barrier, inc=1, device_id={"band": band, "grid": grid}, device_id_type=MESH)
 
     def one(o, c):
-        signal((me + o) % nb, g)
+        n = (w * 4 + g + o) % 32
+        signal(plane * 8 + n // 4, n % 4)
         return c
 
     signal((me + 1) % nb, (g + 2) % 4)
     signal((me + nb - 1) % nb, (g + 2) % 4)
+    lax.fori_loop(1, 32, one, 0)
     for o in range(1, 4):
-        signal(me, (g + o) % 4)
-    lax.fori_loop(1, nb, one, 0)
-    pl.semaphore_wait(barrier, nb + 4)
+        signal((me + 8 * o) % nb, g)
+    pl.semaphore_wait(barrier, 36)
 
 
 def span(start, size):
@@ -142,79 +142,70 @@
     return (n + 2 * (g // 2)) % 4
 
 
-def scatter_groups(src, buf, send, recv, nb, me, g, rows=32, at=0):
+def scatter_slices(src3, buf3, base, send, recv, me, g):
+    plane, w = me // 8, me % 8
+
     def one(o, c):
-        dst = (me + o) % nb
-
-        @pl.when(dst < GROUPS)
-        def _():
-            rcopy(src.at[span(dst * rows, rows)], buf.at[span(me * 32 + at, rows)], send, recv, dst, g).start()
-
+        dst = (w + o) % 8
+        rcopy(
+            src3.at[pl.ds(dst * 27, 27)], buf3.at[pl.ds(base + w * 27, 27)], send, recv, plane * 8 + dst, g
+        ).start()
         return c
 
-    lax.fori_loop(1, nb, one, 0)
-
-    @pl.when(me < GROUPS)
-    def _():
-        buf[span(me * 32 + at, rows), :] = src[span(me * rows, rows), :]
-
-
-def sent_all(ref, sem, me, unit):
-    @pl.when(me < GROUPS)
-    def _():
-        landed(ref.at[0 : (GROUPS - 1) * unit], sem)
-
-    @pl.when(me >= GROUPS)
-    def _():
-        landed(ref.at[0 : GROUPS * unit], sem)
-
-
-def margin_tail(nb, me, g, out_ref, obuf, vbuf, amat, bmat, mt8, red, gsum, rs, rr, gs, gr):
-    @pl.when(me < GROUPS)
-    def _():
-        for c in range(8):
+    lax.fori_loop(1, 8, one, 0)
+    buf3[pl.ds(base + w * 27, 27)] = src3[pl.ds(w * 27, 27)]
+
+
+def lay_orbitals(obuf, bmat):
+    flat = obuf.reshape(3456, 128)
+
+    def chunk(c, carry):
+        for z in range(4):
             for b in range(4):
-                amat[c * 128 + b * 32 : c * 128 + b * 32 + 32, :] = vbuf[pl.ds(b * 8 + c, 32, stride=32), :]
-                bmat[pl.ds(c * 128 + b, 32, stride=4), :] = obuf[pl.ds(c * 4 + b, 32, stride=32), :]
-        m = jnp.zeros((128, 128), F32)
-        for c in range(8):
-            part = slice(c * 128, c * 128 + 128)
-            m = m + lax.dot_general(
-                amat[part, :], bmat[part, :], (((1,), (1,)), ((), ())), precision=HIGHEST, preferred_element_type=F32
-            )
-        m = m * (1.0 / NCELL)
-        mt8[...] = jnp.zeros_like(mt8)
-        for n in range(4):
-            mt8[pl.ds(nth(g, n + 2), 32, stride=8), :] = m[n * 32 : n * 32 + 32, :]
-
-        def one(o, c):
-            dst = (me + o) % nb
-            rcopy(mt8.at[span(dst * 8, 8)], red.at[span(me * 8, 8)], rs, rr, dst, g).start()
-            return c
-
-        lax.fori_loop(1, nb, one, 0)
-        red[span(me * 8, 8), :] = mt8[span(me * 8, 8), :]
-
-    sent_all(red, rr, me, 8)
-    total = red[0:8, :]
-    for s in range(1, GROUPS):
-        total = total + red[s * 8 : s * 8 + 8, :]
-    mine = span(g * 8, 8)
-    gsum[mine, :] = total
-    sends = [rcopy(gsum.at[mine], gsum.at[mine], gs.at[o - 1], gr.at[o - 1], me, (g + o) % 4) for o in range(1, 4)]
-    for s in sends:
-        s.start()
-    for s in sends:
-        s.wait()
-    full = gsum[0:8, :] + gsum[8:16, :] + gsum[16:24, :] + gsum[24:32, :]
-    picked = jnp.zeros((4, 32), F32)
+                bmat[pl.ds(c * 128 + z * 32 + b, 8, stride=4), :] = flat[pl.ds(z * 864 + c * 4 + b, 8, stride=108), :]
+        return carry
+
+    lax.fori_loop(0, 27, chunk, 0)
+
+
+def margin_tail(me, g, out_ref, vbuf, bmat, mt8, red, rs, rr):
+    plane, w = me // 8, me % 8
+    flat = vbuf.reshape(864, 128)
+    m = jnp.zeros((32, 128), F32)
+    dims = (((1,), (1,)), ((), ()))
+    for c in range(27):
+        a = jnp.concatenate([flat[pl.ds(c * 4 + b, 8, stride=108), :] for b in range(4)], axis=0)
+        ah, al = hilo(a)
+        bh, bl = hilo(bmat[c * 128 : c * 128 + 128, :])
+        m = m + (
+            lax.dot_general(ah, bh, dims, preferred_element_type=F32)
+            + lax.dot_general(al, bh, dims, preferred_element_type=F32)
+            + lax.dot_general(ah, bl, dims, preferred_element_type=F32)
+        )
+    m = m * (1.0 / NCELL)
+    lane = lax.broadcasted_iota(jnp.int32, (8, 128), 1) // 32
     for t in range(4):
-        picked = picked + jnp.where(g == t, 1.0, 0.0) * full[0:4, t * 32 : t * 32 + 32]
-    out_ref[...] = picked
-
-    @pl.when(me < GROUPS)
-    def _():
-        landed(mt8.at[0 : 31 * 8], rs)
+        piece = jnp.zeros((8, 128), F32)
+        for b in range(4):
+            row = m[b * 8 : b * 8 + 8, :]
+            turn = 32 * ((b - t) % 4)
+            piece = jnp.where(lane == b, pltpu.roll(row, turn, 1) if turn else row, piece)
+        mt8[pl.ds(t * 64, 8, stride=8), :] = piece
+    here = (g * 8 + w) * 8
+
+    def one(o, c):
+        n = (w * 4 + g + o) % 32
+        dst, to = n // 4, n % 4
+        rcopy(mt8.at[span((to * 8 + dst) * 8, 8)], red.at[span(here, 8)], rs, rr, plane * 8 + dst, to).start()
+        return c
+
+    lax.fori_loop(1, 32, one, 0)
+    red[span(here, 8), :] = mt8[span(here, 8), :]
+    landed(red.at[0 : 31 * 8], rr)
+    total = jnp.sum(red[pl.ds(0, 32, stride=8), :], axis=0, keepdims=True)
+    for b in range(4):
+        out_ref[b : b + 1, :] = total[:, b * 32 : b * 32 + 32]
+    landed(mt8.at[0 : 31 * 8], rs)
 
 
 OWN_I = ((0, 0, 1), (0, 1, 0), (2, 2, 3), (2, 3, 0))
@@ -230,9 +221,9 @@
 
 
 def whole_kernel(nb, mine, w_hbm, v_hbm, wt_hbm, hx_hbm, k_hbm, vec_out, m_out, *scratch):
-    (w_ref, v_ref, wt_ref, hx_ref, k_ref, own, low, a_ref, u_ref, s_ref, t_ref, r_ref, un, on, ow, sb, xr, stage) = scratch[:18]
-    (obuf, vbuf, amat, bmat, mt8, red, gsum, tab, sib_s, sib_r, cross_s, cross_r, fwd_s, fwd_r) = scratch[18:32]
-    (low_s, low_r, ow_s, ow_r, sb_s, sb_r, xr_s, xr_r, os, orr, vs, vr, vs2, vr2, rs, rr, gs, gr) = scratch[32:]
+    (w_ref, v_ref, wt_ref, hx_ref, k_ref, own, low, a_ref, u_ref, s_ref, t_ref, r_ref, un, on, ow, sb, xr) = scratch[:17]
+    (obuf, vbuf, bmat, mt8, red, tab, sib_s, sib_r, cross_s, cross_r, fwd_s, fwd_r) = scratch[17:29]
+    (low_s, low_r, ow_s, ow_r, sb_s, sb_r, xr_s, xr_r, os, orr, vs, vr, zs, zr, rs, rr) = scratch[29:]
     me, g = lax.axis_index("band"), lax.axis_index("grid")
     c, s = (g + 2) % 4, g + 1 - 2 * (g % 2)
     cs = (s + 2) % 4
@@ -353,17 +344,34 @@
         un[part, :] = un[part, :] + sb[at * 216 : at * 216 + 216, :]
         away[n].start()
 
+    plane = me // 8
+    above, below = (me + 8) % nb, (me + nb - 8) % nb
+    pu, pd = (plane + 1) % 4, (plane + 3) % 4
+    along = []
+    for n, (rows, to) in enumerate(
+        (
+            (pl.ds(plane * 216, 216), above),
+            (pl.ds(plane * 216, 216), below),
+            (pl.ds(pd * 216, 108), above),
+            (pl.ds(pu * 216 + 108, 108), below),
+        )
+    ):
+        along.append(rcopy(obuf.at[rows], obuf.at[rows], zs.at[n], zr.at[n], to, g))
+
     def step(n, carry):
         @pl.when(n == 1)
         def _():
             crossed(2)
             landed(low, low_r)
             lay(4, low, 0)
-            scatter_groups(mine, obuf, os, orr, nb, me, g)
+            scatter_slices(mine3, obuf, plane * 216, os, orr, me, g)
 
         @pl.when(n == 2)
         def _():
             crossed(3)
+            landed(obuf.at[0:189], orr)
+            along[0].start()
+            along[1].start()
 
         @pl.when(n == 3)
         def _():
@@ -371,6 +379,13 @@
             forwarded(3)
             lay_band(2)
             lay_band(3)
+
+        @pl.when(n == 5)
+        def _():
+            landed(obuf.at[0:216], zr.at[0])
+            landed(obuf.at[0:216], zr.at[1])
+            along[2].start()
+            along[3].start()
 
         @pl.when(n == 6)
         def _():
@@ -417,7 +432,7 @@
         part = span(g * 864 + q * 216, 216)
         un[part, :] = un[part, :] + ow[span(q * 216, 216), :]
 
-    def finish(n, at, rows):
+    def finish(n):
         b = nth(g, n)
         landed(sb.at[(n * 2 + 1) * 216 : (n * 2 + 2) * 216], sb_r.at[n * 2 + 1])
         landed(xr.at[n * 216 : n * 216 + 216], xr_r.at[n])
@@ -429,7 +444,6 @@
                 + xr[span(n * 216 + t * 8, 8), :]
             )
             vec_out[pl.ds(t * 32 + b, 8, stride=4), :] = value
-            stage[span(rows + t * 16 + at * 8, 8), :] = value
             return carry
 
         lax.fori_loop(0, 27, group, 0)
@@ -440,28 +454,23 @@
     add_owed(1, c)
     send_away(0)
     send_away(1)
+    landed(obuf.at[0:108], zr.at[2])
+    landed(obuf.at[0:108], zr.at[3])
+    lay_orbitals(obuf, bmat)
     add_owed(2, s)
     pass_on[1].start()
     pass_on[3].start()
-    finish(2, 0, 0)
-    finish(3, 1, 0)
-    scatter_groups(stage.at[0:432], vbuf, vs, vr, nb, me, g, 16, 0)
+    finish(2)
+    finish(3)
     add_owed(3, g)
-    finish(0, 0, 432)
-    finish(1, 1, 432)
-    scatter_groups(stage.at[432:864], vbuf, vs2, vr2, nb, me, g, 16, 16)
-
-    @pl.when(me < GROUPS)
-    def _():
-        landed(obuf.at[0 : 31 * 32], orr)
-        landed(vbuf.at[0 : 31 * 16], vr)
-        landed(vbuf.at[0 : 31 * 16], vr2)
-
-    margin_tail(nb, me, g, m_out, obuf, vbuf, amat, bmat, mt8, red, gsum, rs, rr, gs, gr)
-    sent_all(obuf, os, me, 32)
-    sent_all(obuf, vs, me, 16)
-    sent_all(obuf, vs2, me, 16)
-    for copy in cross + fwd + sib + back + pass_on + away:
+    finish(0)
+    finish(1)
+    scatter_slices(vec_out.reshape(216, 4, 128), vbuf, 0, vs, vr, me, g)
+    landed(vbuf.at[0:189], vr)
+    margin_tail(me, g, m_out, vbuf, bmat, mt8, red, rs, rr)
+    landed(vbuf.at[0:189], os)
+    landed(vbuf.at[0:189], vs)
+    for copy in cross + fwd + sib + back + pass_on + away + along:
         copy.wait_send()
     landed(on, low_s)
 
@@ -488,12 +497,12 @@
         scratch_shapes=[b16(1152, 384), b16(1152, 384), b16(1152, 384), b16(48, 144), f32(288, 384)]
         + [f32(3456, 128), f32(864, 128), f32(5, 288, 384), f32(5, 288, 384)]
         + [b16(288, 768), f32(288, 384), b16(1152, 384)]
-        + [f32(3456, 128), f32(864, 128), f32(864, 128), f32(1728, 128), f32(864, 128), f32(864, 128)]
-        + [f32(1024, 128), f32(1024, 128), f32(1024, 128), f32(1024, 128), f32(256, 128), f32(256, 128), f32(32, 128)]
+        + [f32(3456, 128), f32(864, 128), f32(864, 128), f32(1728, 128), f32(864, 128)]
+        + [f32(864, 4, 128), f32(216, 4, 128), f32(3456, 128), f32(256, 128), f32(256, 128)]
         + [dma((8,)), dma((4,)), dma((4,)), dma((4,)), dma((4,)), dma((4,)), dma((4,)), dma, dma]
         + [dma((4,)), dma((4,)), dma((8,)), dma((8,)), dma((4,)), dma((4,))]
-        + [dma] * 8
-        + [dma((3,)), dma((3,))],
+        + [dma] * 4
+        + [dma((4,)), dma((4,)), dma, dma],
         compiler_params=pltpu.CompilerParams(
             collective_id=3, has_side_effects=True, vmem_limit_bytes=60 * 1024 * 1024
         ),

time: 78.4 us -> 79 us (level)
  no operation moved by 1% of the time
where the time goes in v4:
time: 79 us; the launch traced here: 78.8 us
  Pallas kernels  75.8 us (96%)
  local copies, waits for them, and re-layouts  2.39 us (3%)
    pallas_call x1, Pallas kernels, on_device(): pl.pallas_call(functools.partial(whole_kernel, nb), out_shape=(jax.ShapeD...  75.8 us
    unnamed x4, local copies, waits for them, and re-layouts  2.39 us

profile of v4, /device:TPU:1, one launch (start us, length us, event | category | flops | bytes accessed | tf_op | source)
XLA Modules:
  0.0 78.8 jit_solution(8211186450346719884)
XLA Ops:
  0.6 75.8 %shard_map.77 = (f32[864,128]{1,0:T(8,128)}, f32[4,32]{1,0:T(4,128)}) custom-call(f32[864,128]{1,0:T(8,128)} %bitcast.12, bf16[768,384]{1,0:T(8,128)(2,1)} %constant.10.clone.w_hbm, bf16[768,384]{1,0:T(8,128)(2,1)} %constant.11.clone.v_hbm, bf16[768,384]{1,0:T(8,128)(2,1)} %constant.12.clone.wt_hbm, bf16[48,144]{1,0:T(8,128)(2,1)} %constant.13.clone.hx_hbm, ...), custom_call_target="tpu_custom_call" | custom-call | tf_op jit(solution)/shard_map/pallas_call | solution.py:492
  76.4 0.0 copy-start
  76.4 1.8 %copy.12 = f32[4,27648]{1,0:T(4,128)} copy(f32[4,27648]{1,0:T(4,128)} %bitcast.11) | data formatting | bytes 884736
  78.2 0.0 copy-done
  78.2 0.6 copy.13
Async XLA Ops:
  76.4 1.8 %copy-start = (f32[4,32]{1,0:T(4,128)S(1)}, f32[4,32]{1,0:T(4,128)}, u32[]{:S(2)}) copy-start(f32[4,32]{1,0:T(4,128)} %get-tuple-element.5) | copy-start | bytes 1540

commit v5 on v4

--- a/solution.py
+++ b/solution.py
@@ -148,35 +148,50 @@
     def one(o, c):
         dst = (w + o) % 8
         rcopy(
-            src3.at[pl.ds(dst * 27, 27)], buf3.at[pl.ds(base + w * 27, 27)], send, recv, plane * 8 + dst, g
+            src3.at[pl.ds(dst * 27, 27)],
+            buf3.at[pl.ds(base + w * 27, 27)],
+            send,
+            recv,
+            plane * 8 + dst,
+            (g + 2) % 4,
         ).start()
         return c
 
-    lax.fori_loop(1, 8, one, 0)
-    buf3[pl.ds(base + w * 27, 27)] = src3[pl.ds(w * 27, 27)]
-
-
-def lay_orbitals(obuf, bmat):
+    lax.fori_loop(0, 8, one, 0)
+
+
+def lay_orbitals(obuf, line, bh, bl):
     flat = obuf.reshape(3456, 128)
 
-    def chunk(c, carry):
-        for z in range(4):
-            for b in range(4):
-                bmat[pl.ds(c * 128 + z * 32 + b, 8, stride=4), :] = flat[pl.ds(z * 864 + c * 4 + b, 8, stride=108), :]
+    def chunks(p, carry):
+        for h in range(2):
+            c = jnp.minimum(2 * p + h, 26)
+            for z in range(4):
+                for b in range(4):
+                    line[pl.ds(h * 128 + z * 32 + b, 8, stride=4), :] = flat[
+                        pl.ds(z * 864 + c * 4 + b, 8, stride=108), :
+                    ]
+            hi, lo = hilo(line[h * 128 : h * 128 + 128, :])
+            bh[span(p * 128, 128), h * 128 : h * 128 + 128] = hi
+            bl[span(p * 128, 128), h * 128 : h * 128 + 128] = lo
         return carry
 
-    lax.fori_loop(0, 27, chunk, 0)
-
-
-def margin_tail(me, g, out_ref, vbuf, bmat, mt8, red, rs, rr):
+    lax.fori_loop(0, 14, chunks, 0)
+
+
+def margin_tail(me, g, out_ref, vbuf, bh_ref, bl_ref, mt8, red, rs, rr):
     plane, w = me // 8, me % 8
     flat = vbuf.reshape(864, 128)
     m = jnp.zeros((32, 128), F32)
     dims = (((1,), (1,)), ((), ()))
-    for c in range(27):
-        a = jnp.concatenate([flat[pl.ds(c * 4 + b, 8, stride=108), :] for b in range(4)], axis=0)
-        ah, al = hilo(a)
-        bh, bl = hilo(bmat[c * 128 : c * 128 + 128, :])
+    for p in range(14):
+        parts = [
+            jnp.concatenate([flat[pl.ds(c * 4 + b, 8, stride=108), :] for b in range(4)], axis=0)
+            for c in range(2 * p, min(2 * p + 2, 27))
+        ]
+        ah, al = hilo(jnp.concatenate(parts, axis=1))
+        width = 128 * len(parts)
+        bh, bl = bh_ref[p * 128 : p * 128 + 128, 0:width], bl_ref[p * 128 : p * 128 + 128, 0:width]
         m = m + (
             lax.dot_general(ah, bh, dims, preferred_element_type=F32)
             + lax.dot_general(al, bh, dims, preferred_element_type=F32)
@@ -222,8 +237,8 @@
 
 def whole_kernel(nb, mine, w_hbm, v_hbm, wt_hbm, hx_hbm, k_hbm, vec_out, m_out, *scratch):
     (w_ref, v_ref, wt_ref, hx_ref, k_ref, own, low, a_ref, u_ref, s_ref, t_ref, r_ref, un, on, ow, sb, xr) = scratch[:17]
-    (obuf, vbuf, bmat, mt8, red, tab, sib_s, sib_r, cross_s, cross_r, fwd_s, fwd_r) = scratch[17:29]
-    (low_s, low_r, ow_s, ow_r, sb_s, sb_r, xr_s, xr_r, os, orr, vs, vr, zs, zr, rs, rr) = scratch[29:]
+    (obuf, vbuf, line, bh, bl, mt8, red, tab, sib_s, sib_r, cross_s, cross_r, fwd_s, fwd_r) = scratch[17:31]
+    (low_s, low_r, ow_s, ow_r, sb_s, sb_r, xr_s, xr_r, os, orr, vs, vr, zs, zr, rs, rr) = scratch[31:]
     me, g = lax.axis_index("band"), lax.axis_index("grid")
     c, s = (g + 2) % 4, g + 1 - 2 * (g % 2)
     cs = (s + 2) % 4
@@ -369,9 +384,6 @@
         @pl.when(n == 2)
         def _():
             crossed(3)
-            landed(obuf.at[0:189], orr)
-            along[0].start()
-            along[1].start()
 
         @pl.when(n == 3)
         def _():
@@ -379,13 +391,9 @@
             forwarded(3)
             lay_band(2)
             lay_band(3)
-
-        @pl.when(n == 5)
-        def _():
-            landed(obuf.at[0:216], zr.at[0])
-            landed(obuf.at[0:216], zr.at[1])
-            along[2].start()
-            along[3].start()
+            landed(obuf.at[0:216], orr)
+            along[0].start()
+            along[1].start()
 
         @pl.when(n == 6)
         def _():
@@ -415,6 +423,10 @@
             pass_on[2 * n + 1].start()
         send_away(2)
         send_away(3)
+        landed(obuf.at[0:216], zr.at[0])
+        landed(obuf.at[0:216], zr.at[1])
+        along[2].start()
+        along[3].start()
 
     lax.fori_loop(0, 6, step, 0)
 
@@ -454,9 +466,6 @@
     add_owed(1, c)
     send_away(0)
     send_away(1)
-    landed(obuf.at[0:108], zr.at[2])
-    landed(obuf.at[0:108], zr.at[3])
-    lay_orbitals(obuf, bmat)
     add_owed(2, s)
     pass_on[1].start()
     pass_on[3].start()
@@ -466,10 +475,13 @@
     finish(0)
     finish(1)
     scatter_slices(vec_out.reshape(216, 4, 128), vbuf, 0, vs, vr, me, g)
-    landed(vbuf.at[0:189], vr)
-    margin_tail(me, g, m_out, vbuf, bmat, mt8, red, rs, rr)
-    landed(vbuf.at[0:189], os)
-    landed(vbuf.at[0:189], vs)
+    landed(obuf.at[0:108], zr.at[2])
+    landed(obuf.at[0:108], zr.at[3])
+    lay_orbitals(obuf, line, bh, bl)
+    landed(vbuf, vr)
+    margin_tail(me, g, m_out, vbuf, bh, bl, mt8, red, rs, rr)
+    landed(vbuf, os)
+    landed(vbuf, vs)
     for copy in cross + fwd + sib + back + pass_on + away + along:
         copy.wait_send()
     landed(on, low_s)
@@ -498,7 +510,7 @@
         + [f32(3456, 128), f32(864, 128), f32(5, 288, 384), f32(5, 288, 384)]
         + [b16(288, 768), f32(288, 384), b16(1152, 384)]
         + [f32(3456, 128), f32(864, 128), f32(864, 128), f32(1728, 128), f32(864, 128)]
-        + [f32(864, 4, 128), f32(216, 4, 128), f32(3456, 128), f32(256, 128), f32(256, 128)]
+        + [f32(864, 4, 128), f32(216, 4, 128), f32(256, 128), b16(1792, 256), b16(1792, 256), f32(256, 128), f32(256, 128)]
         + [dma((8,)), dma((4,)), dma((4,)), dma((4,)), dma((4,)), dma((4,)), dma((4,)), dma, dma]
         + [dma((4,)), dma((4,)), dma((8,)), dma((8,)), dma((4,)), dma((4,))]
         + [dma] * 4

time: 79 us -> 75.6 us (0.957)
  Pallas kernels: 75.8 us -> 72.4 us
    pallas_call x1, Pallas kernels: 75.8 us -> 72.4 us  [on_device(): pl.pallas_call(functools.partial(whole_kernel, nb), out_shape=(jax.ShapeD...]
where the time goes in v5:
time: 75.6 us; the launch traced here: 75.4 us
  Pallas kernels  72.4 us (96%)
  local copies, waits for them, and re-layouts  2.39 us (3%)
    pallas_call x1, Pallas kernels, on_device(): pl.pallas_call(functools.partial(whole_kernel, nb), out_shape=(jax.ShapeD...  72.4 us
    unnamed x4, local copies, waits for them, and re-layouts  2.39 us

profile of v5, /device:TPU:1, one launch (start us, length us, event | category | flops | bytes accessed | tf_op | source)
XLA Modules:
  0.0 75.4 jit_solution(10321625637601384710)
XLA Ops:
  0.6 72.4 %shard_map.77 = (f32[864,128]{1,0:T(8,128)}, f32[4,32]{1,0:T(4,128)}) custom-call(f32[864,128]{1,0:T(8,128)} %bitcast.12, bf16[768,384]{1,0:T(8,128)(2,1)} %constant.10.clone.w_hbm, bf16[768,384]{1,0:T(8,128)(2,1)} %constant.11.clone.v_hbm, bf16[768,384]{1,0:T(8,128)(2,1)} %constant.12.clone.wt_hbm, bf16[48,144]{1,0:T(8,128)(2,1)} %constant.13.clone.hx_hbm, ...), custom_call_target="tpu_custom_call" | custom-call | tf_op jit(solution)/shard_map/pallas_call | solution.py:504
  73.0 0.0 copy-start
  73.0 1.8 %copy.12 = f32[4,27648]{1,0:T(4,128)} copy(f32[4,27648]{1,0:T(4,128)} %bitcast.11) | data formatting | bytes 884736
  74.8 0.0 copy-done
  74.8 0.6 copy.13
Async XLA Ops:
  73.0 1.8 %copy-start = (f32[4,32]{1,0:T(4,128)S(1)}, f32[4,32]{1,0:T(4,128)}, u32[]{:S(2)}) copy-start(f32[4,32]{1,0:T(4,128)} %get-tuple-element.5) | copy-start | bytes 1540

commit v6 on v5

--- a/solution.py
+++ b/solution.py
@@ -38,7 +38,7 @@
         return np.concatenate([hi, lo], axis=0)
 
     hh, hl = split_np(h)
-    hx = np.concatenate([hh, hh, hl], axis=1)
+    hx = np.concatenate([np.concatenate([hh, hh], axis=1), np.concatenate([hl, np.zeros_like(hl)], axis=1)], axis=0)
     return pack(w), pack(v), pack(w.T.copy()), hx, k.astype(np.float32)
 
 
@@ -61,47 +61,69 @@
     )
 
 
-def swap(t_ref, s_ref, pb, left):
-    for p in range(pb):
-        for j in range(3):
-            for m in range(3):
-                r0 = p * 288 + 2 * j * 48
-                e = t_ref[r0 : r0 + 48, 128 * m : 128 * m + 128]
-                o = t_ref[r0 + 48 : r0 + 96, 128 * m : 128 * m + 128]
-                d0 = p * 288 + 2 * m * 48
-                put(s_ref, d0, 48, 128 * j, jnp.where(left, e, pltpu.roll(o, 64, 1)))
-                put(s_ref, d0 + 48, 48, 128 * j, jnp.where(left, pltpu.roll(e, 64, 1), o))
-
-
-def potential(pb, s_ref, t_ref, r_ref, w_ref, v_ref, wt_ref, hx_ref, k_ref):
+def swap(t_ref, s_ref, left):
+    for j in range(3):
+        for m in range(3):
+            r0, d0 = 2 * j * 48, 2 * m * 48
+            e = t_ref[r0 : r0 + 48, 128 * m : 128 * m + 128]
+            o = t_ref[r0 + 48 : r0 + 96, 128 * m : 128 * m + 128]
+            put(s_ref, d0, 48, 128 * j, jnp.where(left, e, pltpu.roll(o, 64, 1)))
+            put(s_ref, d0 + 48, 48, 128 * j, jnp.where(left, pltpu.roll(e, 64, 1), o))
+
+
+def middle(s_ref, t_ref, r_ref, hx_ref, k_ref):
+    def xdot(g, base):
+        y = jnp.dot(hx_ref[...], r_ref[g * 192 + base : g * 192 + base + 96, :], preferred_element_type=F32)
+        return y[0:48] + y[48:96]
+
+    for g in range(3):
+        for h in range(2):
+            z = 2 * g + h
+            hi, lo = hilo(t_ref[z * 48 : z * 48 + 48, :])
+            r_ref[g * 192 : g * 192 + 48, h * 384 : h * 384 + 384] = hi
+            r_ref[g * 192 + 48 : g * 192 + 96, h * 384 : h * 384 + 384] = lo
+    for g in range(3):
+        d = xdot(g, 0)
+        for h in range(2):
+            z = 2 * g + h
+            hi, lo = hilo(d[:, h * 384 : h * 384 + 384] * k_ref[z * 48 : z * 48 + 48, :])
+            r_ref[g * 192 + 96 : g * 192 + 144, h * 384 : h * 384 + 384] = hi
+            r_ref[g * 192 + 144 : g * 192 + 192, h * 384 : h * 384 + 384] = lo
+    for g in range(3):
+        d = xdot(g, 96)
+        for h in range(2):
+            put(s_ref, (2 * g + h) * 48, 48, 0, d[:, h * 384 : h * 384 + 384])
+
+
+def stages(s_ref, t_ref, r_ref, w_ref, v_ref, wt_ref, hx_ref, k_ref):
     left = lax.broadcasted_iota(jnp.int32, (48, 128), 1) < 64
-    t_ref[...] = mm3(s_ref, w_ref)
-    swap(t_ref, s_ref, pb, left)
-    t_ref[...] = mm3(s_ref, v_ref)
-    h2 = hx_ref[:, 0:96]
-    h1 = hx_ref[:, 96:144]
-
-    def xdot(row):
-        return jnp.dot(h2, r_ref[row : row + 96, :], preferred_element_type=F32) + jnp.dot(
-            h1, r_ref[row : row + 48, :], preferred_element_type=F32
-        )
-
-    for i in range(pb * 6):
-        hi, lo = hilo(t_ref[i * 48 : i * 48 + 48, :])
-        r_ref[i * 192 : i * 192 + 48, :] = hi
-        r_ref[i * 192 + 48 : i * 192 + 96, :] = lo
-        z = i % 6
-        d = xdot(i * 192) * k_ref[z * 48 : z * 48 + 48, :]
-        hi, lo = hilo(d)
-        r_ref[i * 192 + 96 : i * 192 + 144, :] = hi
-        r_ref[i * 192 + 144 : i * 192 + 192, :] = lo
-        put(s_ref, i * 48, 48, 0, xdot(i * 192 + 96))
-    t_ref[...] = mm3(s_ref, v_ref)
-    swap(t_ref, s_ref, pb, left)
-    t_ref[...] = mm3(s_ref, wt_ref)
-
-
+
+    def mm(weights):
+        def run():
+            t_ref[...] = mm3(s_ref, weights)
+
+        return run
+
+    def turn():
+        swap(t_ref, s_ref, left)
+
+    def mid():
+        middle(s_ref, t_ref, r_ref, hx_ref, k_ref)
+
+    return [mm(w_ref), turn, mm(v_ref), mid, mm(v_ref), turn, mm(wt_ref)]
+
+
+def potentials(sets, tables_, between=None):
+    lists = [stages(*refs, *tables_) for refs in sets]
+    count = len(lists[0])
+    for n in range(count + len(lists) - 1):
+        if n == 3 and between is not None:
+            between()
+        for p, steps in enumerate(lists):
+            if 0 <= n - p < count:
+                steps[n - p]()
 MESH = pl.DeviceIdType.MESH
+RELAY = 6
 
 
 def rcopy(src, dst, send, recv, band, grid):
@@ -142,22 +164,21 @@
     return (n + 2 * (g // 2)) % 4
 
 
-def scatter_slices(src3, buf3, base, send, recv, me, g):
-    plane, w = me // 8, me % 8
+def slice_copy(src3, at, buf, rows, send, recv, me, g, w):
+    part = src3.at[pl.ds(at * 27, 27)]
+    return rcopy(part, buf.at[pl.ds(rows, 27)], send, recv, me // 8 * 8 + w, g)
+
+
+def scatter_slices(src3, buf3, base, send, recv, me, g, steps):
+    w = me % 8
 
     def one(o, c):
         dst = (w + o) % 8
-        rcopy(
-            src3.at[pl.ds(dst * 27, 27)],
-            buf3.at[pl.ds(base + w * 27, 27)],
-            send,
-            recv,
-            plane * 8 + dst,
-            (g + 2) % 4,
-        ).start()
+        slice_copy(src3, dst, buf3, base + w * 27, send, recv, me, (g + 2) % 4, dst).start()
         return c
 
-    lax.fori_loop(0, 8, one, 0)
+    for first, last in steps:
+        lax.fori_loop(first, last, one, 0)
 
 
 def lay_orbitals(obuf, line, bh, bl):
@@ -223,9 +244,8 @@
     landed(mt8.at[0 : 31 * 8], rs)
 
 
-OWN_I = ((0, 0, 1), (0, 1, 0), (2, 2, 3), (2, 3, 0))
-OWN_J = ((0, 2, 1), (1, 3, 0), (2, 1, 3), (3, 0, 0))
-STEPS = (7, 6, 7, 6)
+OWN_I = ((0, 0, 1), (0, 1, 0), (2, 2, 3), (2, 3, 2))
+OWN_J = ((0, 2, 1), (1, 3, 0), (2, 1, 3), (3, 0, 2))
 
 
 def chosen(g, values):
@@ -236,9 +256,12 @@
 
 
 def whole_kernel(nb, mine, w_hbm, v_hbm, wt_hbm, hx_hbm, k_hbm, vec_out, m_out, *scratch):
-    (w_ref, v_ref, wt_ref, hx_ref, k_ref, own, low, a_ref, u_ref, s_ref, t_ref, r_ref, un, on, ow, sb, xr) = scratch[:17]
-    (obuf, vbuf, line, bh, bl, mt8, red, tab, sib_s, sib_r, cross_s, cross_r, fwd_s, fwd_r) = scratch[17:31]
-    (low_s, low_r, ow_s, ow_r, sb_s, sb_r, xr_s, xr_r, os, orr, vs, vr, zs, zr, rs, rr) = scratch[31:]
+    (w_ref, v_ref, wt_ref, hx_ref, k_ref, own, low, a_ref, u_ref, un, on, ow, sb, xr) = scratch[:14]
+    (obuf, vbuf, line, bh, bl, mt8, red, tab, sib_s, sib_r, cross_s, cross_r, fwd_s, fwd_r) = scratch[14:28]
+    relay, relay_r, onward_s, onward_r = scratch[53:]
+    (low_s, low_r, ow_s, ow_r, sb_s, sb_r, xr_s, xr_r, os, orr, vs, vr, zs, zr, rs, rr) = scratch[28:44]
+    sets = [scratch[44 + 3 * p : 47 + 3 * p] for p in range(3)]
+    shared = (w_ref, v_ref, wt_ref, hx_ref, k_ref)
     me, g = lax.axis_index("band"), lax.axis_index("grid")
     c, s = (g + 2) % 4, g + 1 - 2 * (g % 2)
     cs = (s + 2) % 4
@@ -373,72 +396,64 @@
     ):
         along.append(rcopy(obuf.at[rows], obuf.at[rows], zs.at[n], zr.at[n], to, g))
 
+    def own_slot(slot):
+        return chosen(g, [row[slot] for row in OWN_I]), chosen(g, [row[slot] for row in OWN_J])
+
     def step(n, carry):
         @pl.when(n == 1)
         def _():
+            scatter_slices(mine3, obuf, plane * 216, os, orr, me, g, ((0, 8),))
             crossed(2)
+            crossed(3)
             landed(low, low_r)
             lay(4, low, 0)
-            scatter_slices(mine3, obuf, plane * 216, os, orr, me, g)
-
-        @pl.when(n == 2)
-        def _():
-            crossed(3)
-
-        @pl.when(n == 3)
-        def _():
-            forwarded(2)
-            forwarded(3)
-            lay_band(2)
-            lay_band(3)
-            landed(obuf.at[0:216], orr)
-            along[0].start()
-            along[1].start()
-
-        @pl.when(n == 6)
-        def _():
-            early()
-
-        i, j, other = 0, 4, 1.0
-        for at, slot in ((0, 0), (3, 1), (6, 2)):
-            i = jnp.where(n == at, chosen(g, [row[slot] for row in OWN_I]), i)
-            j = jnp.where(n == at, chosen(g, [row[slot] for row in OWN_J]), j)
-        for at, k in ((1, 0), (2, 1), (4, 2), (5, 3)):
-            i = jnp.where(n == at, nth(g, k), i)
-        other = jnp.where(i == j, 0.0, 1.0)
-        put(s_ref, 0, 288, 0, a_ref[i] * a_ref[j])
-        potential(1, s_ref, t_ref, r_ref, w_ref, v_ref, wt_ref, hx_ref, k_ref)
-        t = t_ref[...]
+
+        pairs = []
+        for p, slot in ((0, 0), (1, 2)):
+            i, j = own_slot(slot)
+            weight = jnp.where((n == 0) & (p == 1) & (g % 2 == 1), 0.0, 1.0)
+            i, j = jnp.where(n == 0, i, nth(g, p)), jnp.where(n == 0, j, 4)
+            pairs.append((i, j, weight, jnp.where(i == j, 0.0, weight)))
+        for p, (i, j, _, _) in enumerate(pairs):
+            put(sets[p][0], 0, 288, 0, a_ref[i] * a_ref[j])
+        potentials(sets[:2], shared)
+        for p, (i, j, one, two) in enumerate(pairs):
+            t = sets[p][1][...]
+            u_ref[i] = u_ref[i] - one * a_ref[j] * t
+            u_ref[j] = u_ref[j] - two * a_ref[i] * t
+        return carry
+
+    lax.fori_loop(0, 2, step, 0)
+
+    forwarded(2)
+    forwarded(3)
+    lay_band(2)
+    lay_band(3)
+    pairs = [(nth(g, 2), 4), (nth(g, 3), 4), own_slot(1)]
+    for p, (i, j) in enumerate(pairs):
+        put(sets[p][0], 0, 288, 0, a_ref[i] * a_ref[j])
+    def pass_orbitals():
+        landed(obuf.at[0:216], orr)
+        along[0].start()
+        along[1].start()
+
+    potentials(sets, shared, pass_orbitals)
+    for p, (i, j) in enumerate(pairs):
+        t = sets[p][1][...]
         u_ref[i] = u_ref[i] - a_ref[j] * t
-        u_ref[j] = u_ref[j] - other * a_ref[i] * t
-        return carry
-
-    def early():
-        unlay(4, on, 0)
-        for copy in back:
-            copy.start()
-        for n in (2, 3):
-            unlay_band(n)
-            pass_on[2 * n].start()
-            pass_on[2 * n + 1].start()
-        send_away(2)
-        send_away(3)
-        landed(obuf.at[0:216], zr.at[0])
-        landed(obuf.at[0:216], zr.at[1])
-        along[2].start()
-        along[3].start()
-
-    lax.fori_loop(0, 6, step, 0)
-
-    @pl.when(g % 2 == 1)
-    def _():
-        early()
-
-    lax.fori_loop(6, chosen(g, STEPS), step, 0)
-
+        u_ref[j] = u_ref[j] - a_ref[i] * t
+
+    unlay(4, on, 0)
+    for copy in back:
+        copy.start()
+    for n in (2, 3):
+        unlay_band(n)
+        pass_on[2 * n].start()
+        pass_on[2 * n + 1].start()
     for n in (0, 1):
         unlay_band(n)
-
+    send_away(2)
+    send_away(3)
     def add_owed(n, q):
         landed(ow.at[span(q * 216, 216)], ow_r.at[n])
         part = span(g * 864 + q * 216, 216)
@@ -469,20 +484,30 @@
     add_owed(2, s)
     pass_on[1].start()
     pass_on[3].start()
+    landed(obuf.at[0:216], zr.at[0])
+    landed(obuf.at[0:216], zr.at[1])
+    along[2].start()
+    along[3].start()
     finish(2)
     finish(3)
     add_owed(3, g)
     finish(0)
     finish(1)
-    scatter_slices(vec_out.reshape(216, 4, 128), vbuf, 0, vs, vr, me, g)
+    vec3, w = vec_out.reshape(216, 4, 128), me % 8
+    slice_copy(vec3, (w + 4) % 8, relay, 0, vs, relay_r, me, c, (w + RELAY) % 8).start()
+    scatter_slices(vec3, vbuf, 0, vs, vr, me, g, ((1, 4), (5, 8), (0, 1)))
+    landed(relay, relay_r)
+    onward = slice_copy(relay, 0, vbuf, (w + 8 - RELAY) % 8 * 27, onward_s, onward_r, me, g, (w + RELAY) % 8)
+    onward.start()
     landed(obuf.at[0:108], zr.at[2])
     landed(obuf.at[0:108], zr.at[3])
     lay_orbitals(obuf, line, bh, bl)
-    landed(vbuf, vr)
+    landed(vbuf.at[0:189], vr)
+    landed(relay, onward_r)
     margin_tail(me, g, m_out, vbuf, bh, bl, mt8, red, rs, rr)
     landed(vbuf, os)
     landed(vbuf, vs)
-    for copy in cross + fwd + sib + back + pass_on + away + along:
+    for copy in cross + fwd + sib + back + pass_on + away + along + [onward]:
         copy.wait_send()
     landed(on, low_s)
 
@@ -506,15 +531,16 @@
         out_shape=(jax.ShapeDtypeStruct((864, 128), F32), jax.ShapeDtypeStruct((4, 32), F32)),
         in_specs=[vm] + [hbm] * 5,
         out_specs=(vm, vm),
-        scratch_shapes=[b16(1152, 384), b16(1152, 384), b16(1152, 384), b16(48, 144), f32(288, 384)]
+        scratch_shapes=[b16(1152, 384), b16(1152, 384), b16(1152, 384), b16(96, 96), f32(288, 384)]
         + [f32(3456, 128), f32(864, 128), f32(5, 288, 384), f32(5, 288, 384)]
-        + [b16(288, 768), f32(288, 384), b16(1152, 384)]
         + [f32(3456, 128), f32(864, 128), f32(864, 128), f32(1728, 128), f32(864, 128)]
         + [f32(864, 4, 128), f32(216, 4, 128), f32(256, 128), b16(1792, 256), b16(1792, 256), f32(256, 128), f32(256, 128)]
         + [dma((8,)), dma((4,)), dma((4,)), dma((4,)), dma((4,)), dma((4,)), dma((4,)), dma, dma]
         + [dma((4,)), dma((4,)), dma((8,)), dma((8,)), dma((4,)), dma((4,))]
         + [dma] * 4
-        + [dma((4,)), dma((4,)), dma, dma],
+        + [dma((4,)), dma((4,)), dma, dma]
+        + [b16(288, 768), f32(288, 384), b16(576, 768)] * 3
+        + [f32(27, 4, 128), dma, dma, dma],
         compiler_params=pltpu.CompilerParams(
             collective_id=3, has_side_effects=True, vmem_limit_bytes=60 * 1024 * 1024
         ),

time: 75.6 us -> 70.9 us (0.938)
  Pallas kernels: 72.4 us -> 67.7 us
    pallas_call x1, Pallas kernels: 72.4 us -> 67.7 us  [on_device(): pl.pallas_call(functools.partial(whole_kernel, nb), out_shape=(jax.ShapeD...]
where the time goes in v6:
time: 70.9 us; the launch traced here: 70.8 us
  Pallas kernels  67.7 us (95%)
  local copies, waits for them, and re-layouts  2.39 us (3%)
    pallas_call x1, Pallas kernels, on_device(): pl.pallas_call(functools.partial(whole_kernel, nb), out_shape=(jax.ShapeD...  67.7 us
    unnamed x4, local copies, waits for them, and re-layouts  2.39 us

profile of v6, /device:TPU:1, one launch (start us, length us, event | category | flops | bytes accessed | tf_op | source)
XLA Modules:
  0.0 70.8 jit_solution(11210715340355876196)
XLA Ops:
  0.6 67.7 %shard_map.77 = (f32[864,128]{1,0:T(8,128)}, f32[4,32]{1,0:T(4,128)}) custom-call(f32[864,128]{1,0:T(8,128)} %bitcast.12, bf16[768,384]{1,0:T(8,128)(2,1)} %constant.10.clone.w_hbm, bf16[768,384]{1,0:T(8,128)(2,1)} %constant.11.clone.v_hbm, bf16[768,384]{1,0:T(8,128)(2,1)} %constant.12.clone.wt_hbm, bf16[96,96]{1,0:T(8,128)(2,1)} %constant.13.clone.hx_hbm, ...), custom_call_target="tpu_custom_call" | custom-call | tf_op jit(solution)/shard_map/pallas_call | solution.py:529
  68.4 0.0 copy-start
  68.4 1.8 %copy.12 = f32[4,27648]{1,0:T(4,128)} copy(f32[4,27648]{1,0:T(4,128)} %bitcast.11) | data formatting | bytes 884736
  70.2 0.0 copy-done
  70.2 0.6 copy.13
Async XLA Ops:
  68.4 1.8 %copy-start = (f32[4,32]{1,0:T(4,128)S(1)}, f32[4,32]{1,0:T(4,128)}, u32[]{:S(2)}) copy-start(f32[4,32]{1,0:T(4,128)} %get-tuple-element.5) | copy-start | bytes 1540

commit v7 on v6

--- a/solution.py
+++ b/solution.py
@@ -213,9 +213,10 @@
         ah, al = hilo(jnp.concatenate(parts, axis=1))
         width = 128 * len(parts)
         bh, bl = bh_ref[p * 128 : p * 128 + 128, 0:width], bl_ref[p * 128 : p * 128 + 128, 0:width]
+        both = lax.dot_general(jnp.concatenate([ah, al], axis=0), bh, dims, preferred_element_type=F32)
         m = m + (
-            lax.dot_general(ah, bh, dims, preferred_element_type=F32)
-            + lax.dot_general(al, bh, dims, preferred_element_type=F32)
+            both[0:32]
+            + both[32:64]
             + lax.dot_general(ah, bl, dims, preferred_element_type=F32)
         )
     m = m * (1.0 / NCELL)
@@ -255,10 +256,10 @@
     return total
 
 
-def whole_kernel(nb, mine, w_hbm, v_hbm, wt_hbm, hx_hbm, k_hbm, vec_out, m_out, *scratch):
+def whole_kernel(nb, mine_hbm, w_hbm, v_hbm, wt_hbm, hx_hbm, k_hbm, vec_hbm, m_out, *scratch):
     (w_ref, v_ref, wt_ref, hx_ref, k_ref, own, low, a_ref, u_ref, un, on, ow, sb, xr) = scratch[:14]
     (obuf, vbuf, line, bh, bl, mt8, red, tab, sib_s, sib_r, cross_s, cross_r, fwd_s, fwd_r) = scratch[14:28]
-    relay, relay_r, onward_s, onward_r = scratch[53:]
+    relay, relay_r, onward_s, onward_r, mine, vec_out, edge = scratch[53:]
     (low_s, low_r, ow_s, ow_r, sb_s, sb_r, xr_s, xr_r, os, orr, vs, vr, zs, zr, rs, rr) = scratch[28:44]
     sets = [scratch[44 + 3 * p : 47 + 3 * p] for p in range(3)]
     shared = (w_ref, v_ref, wt_ref, hx_ref, k_ref)
@@ -266,6 +267,8 @@
     c, s = (g + 2) % 4, g + 1 - 2 * (g % 2)
     cs = (s + 2) % 4
     up, down = (me + 1) % nb, (me + nb - 1) % nb
+    begin = pltpu.make_async_copy(mine_hbm, mine, edge.at[0])
+    begin.start()
     loads = []
     for n, (a, b) in enumerate(((w_hbm, w_ref), (v_hbm, v_ref), (wt_hbm, wt_ref))):
         loads.append(pltpu.make_async_copy(a.at[0:384], b.at[0:384], tab.at[2 * n]))
@@ -275,6 +278,7 @@
     for copy in loads:
         copy.start()
     greet(nb, me, g)
+    begin.wait()
 
     mine3 = mine.reshape(216, 4, 128)
 
@@ -384,20 +388,30 @@
 
     plane = me // 8
     above, below = (me + 8) % nb, (me + nb - 8) % nb
-    pu, pd = (plane + 1) % 4, (plane + 3) % 4
+    pd = (plane + 3) % 4
     along = []
     for n, (rows, to) in enumerate(
         (
             (pl.ds(plane * 216, 216), above),
             (pl.ds(plane * 216, 216), below),
-            (pl.ds(pd * 216, 108), above),
-            (pl.ds(pu * 216 + 108, 108), below),
+            (pl.ds(pd * 216, 216), above),
         )
     ):
         along.append(rcopy(obuf.at[rows], obuf.at[rows], zs.at[n], zr.at[n], to, g))
 
     def own_slot(slot):
         return chosen(g, [row[slot] for row in OWN_I]), chosen(g, [row[slot] for row in OWN_J])
+
+    def own_slot(slot):
+        return chosen(g, [row[slot] for row in OWN_I]), chosen(g, [row[slot] for row in OWN_J])
+
+    def pass_orbitals():
+        landed(obuf.at[0:216], orr)
+        along[0].start()
+
+        @pl.when(me % 8 < 6)
+        def _():
+            along[1].start()
 
     def step(n, carry):
         @pl.when(n == 1)
@@ -408,14 +422,22 @@
             landed(low, low_r)
             lay(4, low, 0)
 
+        @pl.when(n == 2)
+        def _():
+            forwarded(2)
+            forwarded(3)
+            lay_band(2)
+            lay_band(3)
+
         pairs = []
         for p, slot in ((0, 0), (1, 2)):
             i, j = own_slot(slot)
             weight = jnp.where((n == 0) & (p == 1) & (g % 2 == 1), 0.0, 1.0)
-            i, j = jnp.where(n == 0, i, nth(g, p)), jnp.where(n == 0, j, 4)
+            i, j = jnp.where(n == 0, i, nth(g, 2 * n - 2 + p)), jnp.where(n == 0, j, 4)
             pairs.append((i, j, weight, jnp.where(i == j, 0.0, weight)))
         for p, (i, j, _, _) in enumerate(pairs):
             put(sets[p][0], 0, 288, 0, a_ref[i] * a_ref[j])
+
         potentials(sets[:2], shared)
         for p, (i, j, one, two) in enumerate(pairs):
             t = sets[p][1][...]
@@ -423,29 +445,18 @@
             u_ref[j] = u_ref[j] - two * a_ref[i] * t
         return carry
 
-    lax.fori_loop(0, 2, step, 0)
-
-    forwarded(2)
-    forwarded(3)
-    lay_band(2)
-    lay_band(3)
-    pairs = [(nth(g, 2), 4), (nth(g, 3), 4), own_slot(1)]
-    for p, (i, j) in enumerate(pairs):
-        put(sets[p][0], 0, 288, 0, a_ref[i] * a_ref[j])
-    def pass_orbitals():
-        landed(obuf.at[0:216], orr)
-        along[0].start()
-        along[1].start()
-
-    potentials(sets, shared, pass_orbitals)
-    for p, (i, j) in enumerate(pairs):
-        t = sets[p][1][...]
-        u_ref[i] = u_ref[i] - a_ref[j] * t
-        u_ref[j] = u_ref[j] - a_ref[i] * t
+    lax.fori_loop(0, 3, step, 0)
 
     unlay(4, on, 0)
     for copy in back:
         copy.start()
+    pass_orbitals()
+    i, j = own_slot(1)
+    put(sets[0][0], 0, 288, 0, a_ref[i] * a_ref[j])
+    potentials(sets[:1], shared)
+    t = sets[0][1][...]
+    u_ref[i] = u_ref[i] - a_ref[j] * t
+    u_ref[j] = u_ref[j] - a_ref[i] * t
     for n in (2, 3):
         unlay_band(n)
         pass_on[2 * n].start()
@@ -454,6 +465,7 @@
         unlay_band(n)
     send_away(2)
     send_away(3)
+
     def add_owed(n, q):
         landed(ow.at[span(q * 216, 216)], ow_r.at[n])
         part = span(g * 864 + q * 216, 216)
@@ -482,25 +494,30 @@
     send_away(0)
     send_away(1)
     add_owed(2, s)
+
+    @pl.when(me % 8 >= 6)
+    def _():
+        along[1].start()
+
     pass_on[1].start()
     pass_on[3].start()
     landed(obuf.at[0:216], zr.at[0])
-    landed(obuf.at[0:216], zr.at[1])
     along[2].start()
-    along[3].start()
     finish(2)
     finish(3)
     add_owed(3, g)
     finish(0)
     finish(1)
+    keep = pltpu.make_async_copy(vec_out, vec_hbm, edge.at[1])
     vec3, w = vec_out.reshape(216, 4, 128), me % 8
     slice_copy(vec3, (w + 4) % 8, relay, 0, vs, relay_r, me, c, (w + RELAY) % 8).start()
     scatter_slices(vec3, vbuf, 0, vs, vr, me, g, ((1, 4), (5, 8), (0, 1)))
     landed(relay, relay_r)
     onward = slice_copy(relay, 0, vbuf, (w + 8 - RELAY) % 8 * 27, onward_s, onward_r, me, g, (w + RELAY) % 8)
     onward.start()
-    landed(obuf.at[0:108], zr.at[2])
-    landed(obuf.at[0:108], zr.at[3])
+    keep.start()
+    landed(obuf.at[0:216], zr.at[1])
+    landed(obuf.at[0:216], zr.at[2])
     lay_orbitals(obuf, line, bh, bl)
     landed(vbuf.at[0:189], vr)
     landed(relay, onward_r)
@@ -510,6 +527,7 @@
     for copy in cross + fwd + sib + back + pass_on + away + along + [onward]:
         copy.wait_send()
     landed(on, low_s)
+    keep.wait()
 
 
 def on_device(orbitals):
@@ -529,8 +547,8 @@
     vec, margin = pl.pallas_call(
         functools.partial(whole_kernel, nb),
         out_shape=(jax.ShapeDtypeStruct((864, 128), F32), jax.ShapeDtypeStruct((4, 32), F32)),
-        in_specs=[vm] + [hbm] * 5,
-        out_specs=(vm, vm),
+        in_specs=[hbm] * 6,
+        out_specs=(hbm, vm),
         scratch_shapes=[b16(1152, 384), b16(1152, 384), b16(1152, 384), b16(96, 96), f32(288, 384)]
         + [f32(3456, 128), f32(864, 128), f32(5, 288, 384), f32(5, 288, 384)]
         + [f32(3456, 128), f32(864, 128), f32(864, 128), f32(1728, 128), f32(864, 128)]
@@ -540,7 +558,7 @@
         + [dma] * 4
         + [dma((4,)), dma((4,)), dma, dma]
         + [b16(288, 768), f32(288, 384), b16(576, 768)] * 3
-        + [f32(27, 4, 128), dma, dma, dma],
+        + [f32(27, 4, 128), dma, dma, dma, f32(864, 128), f32(864, 128), dma((2,))],
         compiler_params=pltpu.CompilerParams(
             collective_id=3, has_side_effects=True, vmem_limit_bytes=60 * 1024 * 1024
         ),

time: 70.9 us -> 65.9 us (0.929)
  Pallas kernels: 67.7 us -> 62.7 us
    pallas_call x1, Pallas kernels: 67.7 us -> 62.7 us  [on_device(): pl.pallas_call(functools.partial(whole_kernel, nb), out_shape=(jax.ShapeD...]
where the time goes in v7:
time: 65.9 us; the launch traced here: 65.7 us
  Pallas kernels  62.7 us (95%)
  local copies, waits for them, and re-layouts  2.39 us (4%)
    pallas_call x1, Pallas kernels, on_device(): pl.pallas_call(functools.partial(whole_kernel, nb), out_shape=(jax.ShapeD...  62.7 us
    unnamed x4, local copies, waits for them, and re-layouts  2.39 us

profile of v7, /device:TPU:1, one launch (start us, length us, event | category | flops | bytes accessed | tf_op | source)
XLA Modules:
  0.0 65.7 jit_solution(1896037100765299193)
XLA Ops:
  0.6 62.7 %shard_map.77 = (f32[864,128]{1,0:T(8,128)}, f32[4,32]{1,0:T(4,128)}) custom-call(f32[864,128]{1,0:T(8,128)} %bitcast.12, bf16[768,384]{1,0:T(8,128)(2,1)} %constant.10.clone.w_hbm, bf16[768,384]{1,0:T(8,128)(2,1)} %constant.11.clone.v_hbm, bf16[768,384]{1,0:T(8,128)(2,1)} %constant.12.clone.wt_hbm, bf16[96,96]{1,0:T(8,128)(2,1)} %constant.13.clone.hx_hbm, ...), custom_call_target="tpu_custom_call" | custom-call | tf_op jit(solution)/shard_map/pallas_call | solution.py:547
  63.3 0.0 copy-start
  63.3 1.8 %copy.12 = f32[4,27648]{1,0:T(4,128)} copy(f32[4,27648]{1,0:T(4,128)} %bitcast.11) | data formatting | bytes 884736
  65.2 0.0 copy-done
  65.2 0.6 copy.13
Async XLA Ops:
  63.3 1.8 %copy-start = (f32[4,32]{1,0:T(4,128)S(1)}, f32[4,32]{1,0:T(4,128)}, u32[]{:S(2)}) copy-start(f32[4,32]{1,0:T(4,128)} %get-tuple-element.5) | copy-start | bytes 1540

commit v8 on v7

--- a/solution.py
+++ b/solution.py
@@ -164,17 +164,25 @@
     return (n + 2 * (g // 2)) % 4
 
 
-def slice_copy(src3, at, buf, rows, send, recv, me, g, w):
-    part = src3.at[pl.ds(at * 27, 27)]
+def half_of(w):
+    return (w // 2 + w) % 2
+
+
+def slice_copy(src3, to, buf, rows, send, recv, me, g, w):
+    part = src3.at[pl.ds((to // 2 + 4 * half_of(to)) * 27, 27)]
     return rcopy(part, buf.at[pl.ds(rows, 27)], send, recv, me // 8 * 8 + w, g)
 
 
-def scatter_slices(src3, buf3, base, send, recv, me, g, steps):
+def scatter_slices(src3, buf3, base, send, recv, me, g, steps, half=None):
     w = me % 8
 
     def one(o, c):
         dst = (w + o) % 8
-        slice_copy(src3, dst, buf3, base + w * 27, send, recv, me, (g + 2) % 4, dst).start()
+
+        @pl.when(True if half is None else half_of(dst) == half)
+        def _():
+            slice_copy(src3, dst, buf3, base + w * 27, send, recv, me, (g + 2) % 4, dst).start()
+
         return c
 
     for first, last in steps:
@@ -236,7 +244,8 @@
         rcopy(mt8.at[span((to * 8 + dst) * 8, 8)], red.at[span(here, 8)], rs, rr, plane * 8 + dst, to).start()
         return c
 
-    lax.fori_loop(1, 32, one, 0)
+    for first, last in ((12, 21), (1, 12), (21, 32)):
+        lax.fori_loop(first, last, one, 0)
     red[span(here, 8), :] = mt8[span(here, 8), :]
     landed(red.at[0 : 31 * 8], rr)
     total = jnp.sum(red[pl.ds(0, 32, stride=8), :], axis=0, keepdims=True)
@@ -374,30 +383,48 @@
             pass_on.append(
                 rcopy(cells(un, nth(g, n), q), sb.at[at * 216 : at * 216 + 216], sb_s.at[at], sb_r.at[at], me, s)
             )
-    away = [
-        rcopy(cells(un, nth(g, n), c), xr.at[(n ^ 2) * 216 : (n ^ 2) * 216 + 216], xr_s.at[n], xr_r.at[n ^ 2], me, c)
-        for n in range(4)
-    ]
+    def away_copy(n, first, size, sem):
+        b, at = nth(g, n), (n ^ 2) * 216 + first
+        src = un.at[span(b * 864 + c * 216 + first, size)]
+        return rcopy(src, xr.at[at : at + size], xr_s.at[sem], xr_r.at[sem ^ 2], me, c)
+
+    late = {(n, h): away_copy(n, 112 * h, 112 - 8 * h, n + 4 * h) for n in (0, 1) for h in range(2)}
+    away = {n: away_copy(n, 0, 216, n) for n in (2, 3)}
+
+    def gathered(n, first, size):
+        at = n * 432 + first
+        part = span(nth(g, n) * 864 + c * 216 + first, size)
+        un[part, :] = un[part, :] + sb[at : at + size, :]
 
     def send_away(n):
-        at = n * 2
-        landed(sb.at[at * 216 : at * 216 + 216], sb_r.at[at])
-        part = span(nth(g, n) * 864 + c * 216, 216)
-        un[part, :] = un[part, :] + sb[at * 216 : at * 216 + 216, :]
+        landed(sb.at[n * 432 : n * 432 + 216], sb_r.at[2 * n])
+        gathered(n, 0, 216)
         away[n].start()
+
+    def send_away_part(n, h):
+        if h == 0:
+            landed(sb.at[n * 432 : n * 432 + 216], sb_r.at[2 * n])
+        gathered(n, 112 * h, 112 - 8 * h)
+        late[n, h].start()
 
     plane = me // 8
     above, below = (me + 8) % nb, (me + nb - 8) % nb
-    pd = (plane + 3) % 4
+    pu, pd = (plane + 1) % 4, (plane + 3) % 4
     along = []
-    for n, (rows, to) in enumerate(
+    for n, (first, size, to) in enumerate(
         (
-            (pl.ds(plane * 216, 216), above),
-            (pl.ds(plane * 216, 216), below),
-            (pl.ds(pd * 216, 216), above),
+            (plane * 216, 108, above),
+            (plane * 216 + 108, 108, above),
+            (plane * 216, 216, below),
+            (pd * 216, 108, above),
+            (pd * 216 + 108, 108, above),
+            (pu * 216 + 108, 108, below),
         )
     ):
-        along.append(rcopy(obuf.at[rows], obuf.at[rows], zs.at[n], zr.at[n], to, g))
+        rows = obuf.at[pl.ds(first, size)]
+        along.append(rcopy(rows, rows, zs.at[min(n, 4)], zr.at[min(n, 4)], to, g))
+    last_row = me % 8 >= 6
+    not_last = me % 8 < 6
 
     def own_slot(slot):
         return chosen(g, [row[slot] for row in OWN_I]), chosen(g, [row[slot] for row in OWN_J])
@@ -408,10 +435,11 @@
     def pass_orbitals():
         landed(obuf.at[0:216], orr)
         along[0].start()
-
-        @pl.when(me % 8 < 6)
+        along[1].start()
+
+        @pl.when(not_last)
         def _():
-            along[1].start()
+            along[2].start()
 
     def step(n, carry):
         @pl.when(n == 1)
@@ -471,10 +499,8 @@
         part = span(g * 864 + q * 216, 216)
         un[part, :] = un[part, :] + ow[span(q * 216, 216), :]
 
-    def finish(n):
+    def finish(n, first, last):
         b = nth(g, n)
-        landed(sb.at[(n * 2 + 1) * 216 : (n * 2 + 2) * 216], sb_r.at[n * 2 + 1])
-        landed(xr.at[n * 216 : n * 216 + 216], xr_r.at[n])
 
         def group(t, carry):
             value = (
@@ -485,46 +511,72 @@
             vec_out[pl.ds(t * 32 + b, 8, stride=4), :] = value
             return carry
 
-        lax.fori_loop(0, 27, group, 0)
+        lax.fori_loop(first, last, group, 0)
 
     add_owed(0, cs)
     pass_on[0].start()
     pass_on[2].start()
     add_owed(1, c)
-    send_away(0)
-    send_away(1)
+    for h in range(2):
+        for n in (0, 1):
+            send_away_part(n, h)
+    landed(obuf.at[0:108], zr.at[0])
+    along[3].start()
     add_owed(2, s)
-
-    @pl.when(me % 8 >= 6)
-    def _():
-        along[1].start()
-
     pass_on[1].start()
     pass_on[3].start()
-    landed(obuf.at[0:216], zr.at[0])
-    along[2].start()
-    finish(2)
-    finish(3)
+
+    @pl.when(last_row)
+    def _():
+        along[2].start()
+        landed(obuf.at[0:108], zr.at[1])
+        along[4].start()
+
+    @pl.when(not_last)
+    def _():
+        landed(obuf.at[0:108], zr.at[1])
+        landed(obuf.at[0:216], zr.at[2])
+        along[5].start()
+
     add_owed(3, g)
-    finish(0)
-    finish(1)
+    for n in (0, 1):
+        landed(sb.at[(n * 2 + 1) * 216 : (n * 2 + 2) * 216], sb_r.at[n * 2 + 1])
+        landed(xr.at[n * 216 : n * 216 + 216], xr_r.at[n])
+        finish(n, 0, 27)
+    for n in (2, 3):
+        landed(sb.at[(n * 2 + 1) * 216 : (n * 2 + 2) * 216], sb_r.at[n * 2 + 1])
     keep = pltpu.make_async_copy(vec_out, vec_hbm, edge.at[1])
     vec3, w = vec_out.reshape(216, 4, 128), me % 8
-    slice_copy(vec3, (w + 4) % 8, relay, 0, vs, relay_r, me, c, (w + RELAY) % 8).start()
-    scatter_slices(vec3, vbuf, 0, vs, vr, me, g, ((1, 4), (5, 8), (0, 1)))
+    around = slice_copy(vec3, (w + 4) % 8, relay, 0, vs, relay_r, me, c, (w + RELAY) % 8)
+    for h in range(2):
+        for n in (2, 3):
+            at = n * 216 + h * 112
+            landed(xr.at[at : at + 112 - 8 * h], xr_r.at[n + 4 * h])
+            finish(n, 14 * h, 14 + 13 * h)
+
+        @pl.when(half_of(w) == h)
+        def _():
+            around.start()
+
+        scatter_slices(vec3, vbuf, 0, vs, vr, me, g, ((3, 4), (5, 6), (1, 3), (6, 8), (0, 1)), h)
     landed(relay, relay_r)
     onward = slice_copy(relay, 0, vbuf, (w + 8 - RELAY) % 8 * 27, onward_s, onward_r, me, g, (w + RELAY) % 8)
     onward.start()
     keep.start()
-    landed(obuf.at[0:216], zr.at[1])
-    landed(obuf.at[0:216], zr.at[2])
+
+    @pl.when(last_row)
+    def _():
+        landed(obuf.at[0:216], zr.at[2])
+
+    landed(obuf.at[0:108], zr.at[3])
+    landed(obuf.at[0:108], zr.at[4])
     lay_orbitals(obuf, line, bh, bl)
     landed(vbuf.at[0:189], vr)
     landed(relay, onward_r)
     margin_tail(me, g, m_out, vbuf, bh, bl, mt8, red, rs, rr)
     landed(vbuf, os)
     landed(vbuf, vs)
-    for copy in cross + fwd + sib + back + pass_on + away + along + [onward]:
+    for copy in cross + fwd + sib + back + pass_on + [*late.values(), *away.values()] + along[:5] + [onward]:
         copy.wait_send()
     landed(on, low_s)
     keep.wait()
@@ -554,9 +606,9 @@
         + [f32(3456, 128), f32(864, 128), f32(864, 128), f32(1728, 128), f32(864, 128)]
         + [f32(864, 4, 128), f32(216, 4, 128), f32(256, 128), b16(1792, 256), b16(1792, 256), f32(256, 128), f32(256, 128)]
         + [dma((8,)), dma((4,)), dma((4,)), dma((4,)), dma((4,)), dma((4,)), dma((4,)), dma, dma]
-        + [dma((4,)), dma((4,)), dma((8,)), dma((8,)), dma((4,)), dma((4,))]
+        + [dma((4,)), dma((4,)), dma((8,)), dma((8,)), dma((8,)), dma((8,))]
         + [dma] * 4
-        + [dma((4,)), dma((4,)), dma, dma]
+        + [dma((5,)), dma((5,)), dma, dma]
         + [b16(288, 768), f32(288, 384), b16(576, 768)] * 3
         + [f32(27, 4, 128), dma, dma, dma, f32(864, 128), f32(864, 128), dma((2,))],
         compiler_params=pltpu.CompilerParams(

time: 65.9 us -> 66 us (level)
  no operation moved by 1% of the time
where the time goes in v8:
time: 66 us; the launch traced here: 65.9 us
  Pallas kernels  62.8 us (95%)
  local copies, waits for them, and re-layouts  2.39 us (4%)
    pallas_call x1, Pallas kernels, on_device(): pl.pallas_call(functools.partial(whole_kernel, nb), out_shape=(jax.ShapeD...  62.8 us
    unnamed x4, local copies, waits for them, and re-layouts  2.39 us

profile of v8, /device:TPU:1, one launch (start us, length us, event | category | flops | bytes accessed | tf_op | source)
XLA Modules:
  0.0 65.9 jit_solution(2049434506960631907)
XLA Ops:
  0.6 62.8 %shard_map.77 = (f32[864,128]{1,0:T(8,128)}, f32[4,32]{1,0:T(4,128)}) custom-call(f32[864,128]{1,0:T(8,128)} %bitcast.12, bf16[768,384]{1,0:T(8,128)(2,1)} %constant.10.clone.w_hbm, bf16[768,384]{1,0:T(8,128)(2,1)} %constant.11.clone.v_hbm, bf16[768,384]{1,0:T(8,128)(2,1)} %constant.12.clone.wt_hbm, bf16[96,96]{1,0:T(8,128)(2,1)} %constant.13.clone.hx_hbm, ...), custom_call_target="tpu_custom_call" | custom-call | tf_op jit(solution)/shard_map/pallas_call | solution.py:599
  63.5 0.0 copy-start
  63.5 1.8 %copy.12 = f32[4,27648]{1,0:T(4,128)} copy(f32[4,27648]{1,0:T(4,128)} %bitcast.11) | data formatting | bytes 884736
  65.3 0.0 copy-done
  65.3 0.6 copy.13
Async XLA Ops:
  63.5 1.8 %copy-start = (f32[4,32]{1,0:T(4,128)S(1)}, f32[4,32]{1,0:T(4,128)}, u32[]{:S(2)}) copy-start(f32[4,32]{1,0:T(4,128)} %get-tuple-element.5) | copy-start | bytes 1540

commit v9 on v7

--- a/solution.py
+++ b/solution.py
@@ -256,7 +256,7 @@
     return total
 
 
-def whole_kernel(nb, mine_hbm, w_hbm, v_hbm, wt_hbm, hx_hbm, k_hbm, vec_hbm, m_out, *scratch):
+def whole_kernel(nb, mine_hbm, w_hbm, v_hbm, wt_hbm, hx_hbm, k_hbm, vec_a, vec_b, m_out, *scratch):
     (w_ref, v_ref, wt_ref, hx_ref, k_ref, own, low, a_ref, u_ref, un, on, ow, sb, xr) = scratch[:14]
     (obuf, vbuf, line, bh, bl, mt8, red, tab, sib_s, sib_r, cross_s, cross_r, fwd_s, fwd_r) = scratch[14:28]
     relay, relay_r, onward_s, onward_r, mine, vec_out, edge = scratch[53:]
@@ -508,14 +508,18 @@
     add_owed(3, g)
     finish(0)
     finish(1)
-    keep = pltpu.make_async_copy(vec_out, vec_hbm, edge.at[1])
+    keep = [
+        pltpu.make_async_copy(vec_out.at[0:432], vec_a, edge.at[1]),
+        pltpu.make_async_copy(vec_out.at[432:864], vec_b, edge.at[2]),
+    ]
     vec3, w = vec_out.reshape(216, 4, 128), me % 8
     slice_copy(vec3, (w + 4) % 8, relay, 0, vs, relay_r, me, c, (w + RELAY) % 8).start()
     scatter_slices(vec3, vbuf, 0, vs, vr, me, g, ((1, 4), (5, 8), (0, 1)))
     landed(relay, relay_r)
     onward = slice_copy(relay, 0, vbuf, (w + 8 - RELAY) % 8 * 27, onward_s, onward_r, me, g, (w + RELAY) % 8)
     onward.start()
-    keep.start()
+    for copy in keep:
+        copy.start()
     landed(obuf.at[0:216], zr.at[1])
     landed(obuf.at[0:216], zr.at[2])
     lay_orbitals(obuf, line, bh, bl)
@@ -527,7 +531,8 @@
     for copy in cross + fwd + sib + back + pass_on + away + along + [onward]:
         copy.wait_send()
     landed(on, low_s)
-    keep.wait()
+    for copy in keep:
+        copy.wait()
 
 
 def on_device(orbitals):
@@ -544,11 +549,15 @@
     def b16(*shape):
         return pltpu.VMEM(shape, BF)
 
-    vec, margin = pl.pallas_call(
+    first, second, margin = pl.pallas_call(
         functools.partial(whole_kernel, nb),
-        out_shape=(jax.ShapeDtypeStruct((864, 128), F32), jax.ShapeDtypeStruct((4, 32), F32)),
+        out_shape=(
+            jax.ShapeDtypeStruct((432, 128), F32),
+            jax.ShapeDtypeStruct((432, 128), F32),
+            jax.ShapeDtypeStruct((4, 32), F32),
+        ),
         in_specs=[hbm] * 6,
-        out_specs=(hbm, vm),
+        out_specs=(hbm, hbm, vm),
         scratch_shapes=[b16(1152, 384), b16(1152, 384), b16(1152, 384), b16(96, 96), f32(288, 384)]
         + [f32(3456, 128), f32(864, 128), f32(5, 288, 384), f32(5, 288, 384)]
         + [f32(3456, 128), f32(864, 128), f32(864, 128), f32(1728, 128), f32(864, 128)]
@@ -558,11 +567,12 @@
         + [dma] * 4
         + [dma((4,)), dma((4,)), dma, dma]
         + [b16(288, 768), f32(288, 384), b16(576, 768)] * 3
-        + [f32(27, 4, 128), dma, dma, dma, f32(864, 128), f32(864, 128), dma((2,))],
+        + [f32(27, 4, 128), dma, dma, dma, f32(864, 128), f32(864, 128), dma((3,))],
         compiler_params=pltpu.CompilerParams(
             collective_id=3, has_side_effects=True, vmem_limit_bytes=60 * 1024 * 1024
         ),
     )(mine, w, v, wt, hx, k)
+    vec = jnp.concatenate([first, second], axis=0)
     return vec.reshape(216, 4, 128).transpose(1, 0, 2).reshape(4, 27648), margin.T
 
 

time: 65.9 us -> 65.9 us (level)
  other arithmetic: 0 us -> 1.83 us
  local copies, waits for them, and re-layouts: 2.39 us -> 0.58 us
    concatenate x0 -> x1, other arithmetic: none -> 1.83 us  [on_device(): vec = jnp.concatenate([first, second], axis=0)]
    unnamed x4 -> x3, local copies, waits for them, and re-layouts: 2.39 us -> 0.58 us
where the time goes in v9:
time: 65.9 us; the launch traced here: 65.7 us
  Pallas kernels  62.7 us (95%)
  other arithmetic  1.83 us (3%)
    pallas_call x1, Pallas kernels, on_device(): pl.pallas_call(functools.partial(whole_kernel, nb), out_shape=(jax.ShapeD...  62.7 us
    concatenate x1, other arithmetic, on_device(): vec = jnp.concatenate([first, second], axis=0)  1.83 us

profile of v9, /device:TPU:1, one launch (start us, length us, event | category | flops | bytes accessed | tf_op | source)
XLA Modules:
  0.0 65.7 jit_solution(10892689750859491862)
XLA Ops:
  0.6 62.7 %shard_map.77 = (f32[432,128]{1,0:T(8,128)}, f32[432,128]{1,0:T(8,128)}, f32[4,32]{1,0:T(4,128)}) custom-call(f32[864,128]{1,0:T(8,128)} %bitcast.12, bf16[768,384]{1,0:T(8,128)(2,1)} %constant.10.clone.w_hbm, bf16[768,384]{1,0:T(8,128)(2,1)} %constant.11.clone.v_hbm, bf16[768,384]{1,0:T(8,128)(2,1)} %constant.12.clone.wt_hbm, ...), custom_call_target="tpu_custom_call" | custom-call | tf_op jit(solution)/shard_map/pallas_call | solution.py:552
  63.3 0.0 copy-start
  63.3 1.8 %pad_maximum_fusion = f32[864,128]{1,0:T(8,128)} fusion(f32[432,128]{1,0:T(8,128)} %get-tuple-element.6, f32[432,128]{1,0:T(8,128)} %get-tuple-element.5), kind=kLoop, calls=%fused_computation | loop fusion | flops 110592 | bytes 884736 | tf_op jit(solution)/shard_map/concatenate | solution.py:575
  65.2 0.0 copy-done
  65.2 0.6 copy.11
Async XLA Ops:
  63.3 1.8 %copy-start = (f32[4,32]{1,0:T(4,128)S(1)}, f32[4,32]{1,0:T(4,128)}, u32[]{:S(2)}) copy-start(f32[4,32]{1,0:T(4,128)} %get-tuple-element.7) | copy-start | bytes 1540
